TPU v7x, 128 devices: a whole 4x4x4 slice. The times are simulated.
128 devices in a mesh: freq: 8 (over x, z_hi), panel: 16 (over z_lo, y, core).
Axes of the slice: x: 4, y: 4, z: 4 (z_hi: 2, z_lo: 2; z = z_hi * 2 + z_lo), core: 2. Of those that a mesh axis runs over, the one named last changes fastest.
Arguments:
- traces: bfloat16 [640, 640, 1024], P('panel', 'freq'), may hold values from -6 to 6
- filters: float32 [16, 7, 64], replicated, may hold values from -0.25 to 0.25
Outputs:
- primaries: bfloat16 [640, 640, 1024], P('panel', 'freq')
All inputs are finite; a program needn't handle non-finite values.
Results may differ from a plain program's by a relative error of at most 0.0095.
Values may be sent and summed in bfloat16 or wider, within the bound.
No kernel may reach another device: no remote copies, remote signals or barrier semaphores. Data moves between devices by JAX's collectives and lax.ppermute only.
A program may use at most 128 MiB of HBM per device.

v0:
```python
import math

import jax
import jax.numpy as jnp
from jax import lax
from jax.sharding import PartitionSpec as P

NS = 640
NT = 1024
NF = 96
FLO = 8
TAPS = 64
SPAN = 7
RWIN = 40


def wave_table(freq_bins, sample_index):
    phases = freq_bins[:, None] * sample_index[None, :] % NT
    angles = phases.astype(jnp.float32) * jnp.float32(2.0 * math.pi / NT)
    return (jnp.cos(angles), jnp.sin(angles))


def complex_product(left_side, right_side):

    def factor_product(leading_factor, trailing_factor):
        return jnp.einsum(
            "gjo,god->gjd", leading_factor, trailing_factor, preferred_element_type=jnp.float32
        )

    part_real = factor_product(left_side[0], right_side[0]) - factor_product(
        left_side[1], right_side[1]
    )
    part_imag = factor_product(left_side[0], right_side[1]) + factor_product(
        left_side[1], right_side[0]
    )
    return jnp.stack([part_real, part_imag])


def response(filters, freq_bins):
    tap_index = jnp.arange(TAPS, dtype=jnp.int32)
    cosine_wave, sine_wave = wave_table(freq_bins, tap_index)
    filter_real = jnp.einsum("fk,wjk->fjw", cosine_wave, filters)
    filter_imag = -jnp.einsum("fk,wjk->fjw", sine_wave, filters)
    return (jnp.repeat(filter_real, RWIN, axis=2), jnp.repeat(filter_imag, RWIN, axis=2))


def apply_filter(extended, filter_real, filter_imag, source_count):
    sum_real = jnp.zeros(extended.shape[1:2] + (source_count,) + extended.shape[3:], jnp.float32)
    sum_imag = jnp.zeros_like(sum_real)
    for shifted in range(SPAN):
        part_real = extended[0, :, shifted : shifted + source_count, :]
        part_imag = extended[1, :, shifted : shifted + source_count, :]
        weight_real = filter_real[:, shifted][:, None, :]
        weight_imaginary = filter_imag[:, shifted][:, None, :]
        sum_real = sum_real + weight_real * part_real - weight_imaginary * part_imag
        sum_imag = sum_imag + weight_real * part_imag + weight_imaginary * part_real
    return jnp.stack([sum_real, sum_imag])


def per_device(traces, filters):
    shot_rows, receiver_cols, time_sample_count = traces.shape
    rim_width = SPAN // 2
    scale_sources = jnp.float32(math.sqrt(NS))
    freq_bins = FLO + jnp.arange(NF, dtype=jnp.int32)
    cosine_wave, sine_wave = wave_table(freq_bins, jnp.arange(NT, dtype=jnp.int32))
    forward = (jnp.concatenate([cosine_wave, -sine_wave], 0) / jnp.float32(math.sqrt(NT))).astype(
        jnp.bfloat16
    )
    reciprocal_value = jnp.concatenate([cosine_wave, -sine_wave], 0).astype(jnp.bfloat16)
    spectra = jnp.einsum("srt,ct->csr", traces, forward, preferred_element_type=jnp.float32)
    spectra = spectra.astype(jnp.bfloat16).reshape(2, NF, shot_rows, receiver_cols)
    columns = lax.all_to_all(spectra, "panel", split_axis=1, concat_axis=2, tiled=True)
    slice_count = columns.shape[1]
    first_slice = lax.axis_index("panel") * slice_count
    complete = lax.all_gather(columns, "freq", axis=3, tiled=True)
    order_one = (complex_product(complete, columns) / scale_sources).astype(jnp.bfloat16)
    order_two = complex_product(complete, order_one) / scale_sources
    prediction = (order_one.astype(jnp.float32) - order_two).astype(jnp.bfloat16)
    extended = jnp.pad(
        prediction.astype(jnp.float32), ((0, 0), (0, 0), (rim_width, rim_width), (0, 0))
    )
    own_bins = FLO + first_slice + jnp.arange(slice_count, dtype=jnp.int32)
    filter_real, filter_imag = response(filters, own_bins)
    receiver_start = lax.axis_index("freq") * receiver_cols
    filter_real = lax.dynamic_slice_in_dim(filter_real, receiver_start, receiver_cols, 2)
    filter_imag = lax.dynamic_slice_in_dim(filter_imag, receiver_start, receiver_cols, 2)
    matched = apply_filter(extended, filter_real, filter_imag, NS)
    returned = lax.all_to_all(
        matched.astype(jnp.bfloat16), "panel", split_axis=2, concat_axis=1, tiled=True
    )
    matched_rows = returned.reshape(2 * NF, shot_rows, receiver_cols)
    multiples = jnp.einsum(
        "csr,ct->srt", matched_rows, reciprocal_value, preferred_element_type=jnp.float32
    )
    multiples = multiples / jnp.float32(math.sqrt(NF))
    return (traces.astype(jnp.float32) - multiples).astype(jnp.bfloat16)


def solution(mesh):
    placed = (P("panel", "freq", None), P())
    return jax.shard_map(
        per_device, mesh=mesh, in_specs=placed, out_specs=P("panel", "freq", None), check_vma=False
    )
```

profile of v0, /device:TPU:1, one launch (start us, length us, event | category | flops | bytes accessed | tf_op | source)
XLA Modules:
  0.0 312.2 jit_solution(14349941599640643925)
XLA Ops:
  6.5 1.6 fusion.58
  8.2 0.8 copy-done.4
  8.9 0.2 copy-done.6
  9.1 4.8 %convolution_convert_fusion = bf16[192,40,80]{0,2,1:T(8,128)(2,1)S(1)} fusion(bf16[40,80,1024]{2,1,0:T(8,128)(2,1)} %param.2, f32[96,1024]{1,0:T(8,128)S(1)} %get-tuple-element.24, f32[96,1024]{1,0:T(8,128)S(1)} %get-tuple-element.23), kind=kOutput, calls=%fused_computation.35 | convolution fusion | flops 1259495424 | bytes 8568832 | tf_op jit(solution)/shard_map/srt,ct->csr/dot_general | solution.py:70
  13.9 0.9 reshape.26
  14.7 3.3 %copy.54 = bf16[2,96,40,80]{3,2,0,1:T(8,128)(2,1)} copy(bf16[2,96,40,80]{1,0,3,2:T(2,128)(2,1)S(1)} %reshape.26) | data formatting | bytes 2457600 | tf_op jit(solution)/shard_map/reshape | solution.py:71
  18.1 32.3 %all_to_all.33 = bf16[2,96,40,80]{3,2,0,1:T(8,128)(2,1)S(1)} all-to-all(bf16[2,96,40,80]{3,2,0,1:T(8,128)(2,1)} %copy.54), channel_id=1, replica_groups=mesh['freq'=8,'panel'=16] {'panel'}, dimensions={1} | all-to-all | bytes 2457600 | tf_op jit(solution)/shard_map/all_to_all | solution.py:72
  50.4 1.7 copy.56
  52.2 4.5 %copy.57 = bf16[2,6,640,80]{2,0,1,3:T(2,128)(2,1)} copy(bf16[2,6,640,80]{3,2,1,0:T(8,128)(2,1)} %bitcast.140) | data formatting | bytes 2457600 | tf_op jit(solution)/shard_map/all_to_all | solution.py:72
  56.7 0.0 all-gather.2.cloned.1.call-update
  56.8 0.2 convolution_bitcast_fusion
  57.0 0.2 broadcast_in_dim.4
  57.2 0.2 reshape.25
  57.4 0.2 fusion.45
  57.7 0.2 broadcast_in_dim.5
  57.8 0.2 reshape.27
  58.1 0.2 constant_dynamic-slice_fusion.10
  58.4 0.3 copy.55
  58.7 0.3 fusion.81
  59.1 0.1 copy.62
  59.2 0.1 copy.59
  59.3 118.6 %all-gather.2.cloned.1.call-done = bf16[2,6,640,640]{2,0,1,3:T(2,128)(2,1)} async-done(((bf16[2,6,640,80]{2,0,1,3:T(2,128)(2,1)}), bf16[2,6,640,640]{2,0,1,3:T(2,128)(2,1)}) %all-gather.2.cloned.1.call-update) | async-done | bytes 9830416 | tf_op jit(solution)/shard_map/all_gather | solution.py:75
  177.9 20.6 %fusion.80 = (bf16[1,6,640,640]{2,0,1,3:T(2,128)(2,1)}, bf16[1,6,640,640]{2,0,1,3:T(2,128)(2,1)}) fusion(bf16[2,6,640,640]{2,0,1,3:T(2,128)(2,1)} %all-gather.2.cloned.1.call-done), kind=kLoop, calls=%fused_computation.122 | loop fusion | bytes 19660800 | tf_op jit(solution)/shard_map/slice | solution.py:30
  198.5 19.7 %copy.91 = bf16[1,6,640,640]{3,2,1,0:T(8,128)(2,1)} copy(bf16[1,6,640,640]{2,0,1,3:T(2,128)(2,1)} %get-tuple-element.6) | data formatting | bytes 9830400
  218.3 19.8 %copy.90 = bf16[1,6,640,640]{3,2,1,0:T(8,128)(2,1)} copy(bf16[1,6,640,640]{2,0,1,3:T(2,128)(2,1)} %get-tuple-element.5) | data formatting | bytes 9830400
  238.0 4.2 %fusion.6 = f32[6,640,80]{1,2,0:T(8,128)S(1)} fusion(bf16[6,640,80]{2,1,0:T(8,128)(2,1)S(1)} %bitcast.133, bf16[1,6,640,640]{3,2,1,0:T(8,128)(2,1)} %copy.91), kind=kOutput, calls=%fused_computation.7 | convolution fusion | flops 393216000 | bytes 6758400 | tf_op jit(solution)/shard_map/gjo,god->gjd/dot_general | solution.py:26
  242.2 1.7 fusion.4
  243.9 0.7 copy-done.3
  244.6 1.7 fusion.23
  246.3 1.7 fusion.29
  247.9 0.2 fusion.16
  248.2 1.7 fusion.2
  249.8 1.7 fusion
  251.5 1.7 fusion.35
  253.2 1.7 fusion.41
  254.8 0.4 fusion.44
  255.2 5.4 %subtract_convert_fusion.1 = bf16[1,6,640,80]{2,3,1,0:T(8,128)(2,1)S(1)} fusion(f32[2,6,640,80]{2,3,1,0:T(8,128)S(1)} %fusion.44, f32[6,80]{1,0:T(8,128)S(1)} %bitcast.143, f32[6,80]{1,0:T(8,128)S(1)} %bitcast.145, f32[6,80]{1,0:T(8,128)S(1)} %bitcast.147, f32[6,80]{1,0:T(8,128)S(1)} %bitcast.149, f32[6,80]{1,0:T(8,128)S(1)} %bitcast.151, ...), kind=kLoop, calls=%fused_computation.47 | loop fusion | flops 8601600 | bytes 5586944 | tf_op jit(solution)/shard_map/convert
  260.6 5.3 %add_convert_fusion = bf16[1,6,640,80]{2,3,1,0:T(8,128)(2,1)S(1)} fusion(f32[2,6,640,80]{2,3,1,0:T(8,128)S(1)} %fusion.44, f32[6,80]{1,0:T(8,128)S(1)} %bitcast.144, f32[6,80]{1,0:T(8,128)S(1)} %bitcast.146, f32[6,80]{1,0:T(8,128)S(1)} %bitcast.148, f32[6,80]{1,0:T(8,128)S(1)} %bitcast.150, f32[6,80]{1,0:T(8,128)S(1)} %bitcast.152, ...), kind=kLoop, calls=%fused_computation.46 | loop fusion | flops 8601600 | bytes 5586944 | tf_op jit(solution)/shard_map/convert.1
  265.9 0.1 pad_maximum_fusion
  266.1 2.6 copy.67
  268.6 0.0 slice-start
  268.7 30.9 %all_to_all.34 = bf16[2,6,640,80]{3,0,1,2:T(2,128)(2,1)S(1)} all-to-all(bf16[2,6,640,80]{3,0,1,2:T(2,128)(2,1)S(1)} %copy.67), channel_id=1, replica_groups=mesh['freq'=8,'panel'=16] {'panel'}, dimensions={2} | all-to-all | bytes 2457600 | tf_op jit(solution)/shard_map/all_to_all | solution.py:88
  299.5 0.4 copy.68
  299.9 0.3 copy.69
  300.3 0.9 slice-done.1
  301.2 0.1 copy-done.5
  301.3 0.1 copy-done.7
  301.4 4.0 %subtract_convert_fusion = bf16[40,80,1024]{2,1,0:T(8,128)(2,1)} fusion(bf16[40,80,1024]{2,1,0:T(8,128)(2,1)S(1)} %bitcast.142, bf16[192,40,80]{2,1,0:T(8,128)(2,1)S(1)} %bitcast.138, f32[96,1024]{1,0:T(8,128)S(1)} %copy-done.7, f32[96,1024]{1,0:T(8,128)S(1)} %copy-done.5), kind=kOutput, calls=%fused_computation | convolution fusion | flops 1272184832 | bytes 15122432 | tf_op jit(solution)/shard_map/csr,ct->srt/dot_general | solution.py:92
  (33 shorter events, 0.1 us)
Async XLA Ops:
  6.5 50.2 %copy-start = (f32[16,7,64]{2,0,1:T(8,128)S(1)}, f32[16,7,64]{2,0,1:T(8,128)}, u32[]{:S(2)}) copy-start(f32[16,7,64]{2,0,1:T(8,128)} %param.3) | copy-start | bytes 86020
  6.5 171.3 %all-gather.2.cloned.1.call-start = ((), (), s32[]{:S(2)}) async-start(), calls=%async_computation.2 | async-start | bytes 11059200 | tf_op jit(solution)/shard_map/all_gather | solution.py:75
  8.2 0.8 copy-start.4
  8.2 0.9 copy-start.6
  238.0 4.2 %copy-start.2 = (bf16[1,6,640,640]{3,2,1,0:T(8,128)(2,1)S(1)}, bf16[1,6,640,640]{3,2,1,0:T(8,128)(2,1)}, u32[]{:S(2)}) copy-start(bf16[1,6,640,640]{3,2,1,0:T(8,128)(2,1)} %copy.91) | copy-start | bytes 14745604
  242.2 2.4 copy-start.3
  268.6 31.6 %slice-start = ((s8[6553600]{0:T(1024)(128)(4,1)}), s8[4194304]{0:T(1024)(128)(4,1)S(1)}, s32[]{:S(2)}) async-start(s8[6553600]{0:T(1024)(128)(4,1)} %bitcast.141), calls=%async_computation.3 | async-start | bytes 8388608
  299.5 1.7 slice-start.1
  299.9 1.4 copy-start.5
  299.9 1.5 copy-start.7
  301.4 4.0 %copy-start.1 = (f32[16,7,64]{2,0,1:T(8,128)S(1)}, f32[16,7,64]{2,0,1:T(8,128)}, u32[]{:S(2)}) copy-start(f32[16,7,64]{2,0,1:T(8,128)} %param.3) | copy-start | bytes 86020
Sparse Core Ops, SparseCore 0:
  56.8 120.9 all-gather.1
where the time goes:
time: 314 us; the launch traced here: 312 us
  waiting for transfers between devices  119 us (38%)
  local copies, waits for them, and re-layouts  78.6 us (25%)
  blocking collectives  63.2 us (20%)
  matrix products  25 us (8%)
  between operations  13.7 us (4%)
  other arithmetic  13.1 us (4%)
    all_gather x1, waiting for transfers between devices, per_device(): complete = lax.all_gather(columns, 'freq', axis=3, tiled=True)  119 us
    unnamed x36, local copies, waits for them, and re-layouts  42.4 us
    all_to_all x1, blocking collectives, per_device(): lax.all_to_all(spectra, 'panel', split_axis=1, concat_axis=2, tiled=True)  32.3 us
    all_to_all x1, blocking collectives, per_device(): lax.all_to_all(matched.astype(jnp.bfloat16), 'panel', split_axis=2, conca...  30.9 us
    slice x1, local copies, waits for them, and re-layouts, complex_product(): left_side[0]  20.6 us
    dot_general x8, matrix products, factor_product(): jnp.einsum('gjo,god->gjd', leading_factor, trailing_factor, preferred_ele...  15.8 us
    another operation x2, other arithmetic  10.7 us
    all_to_all x3, local copies, waits for them, and re-layouts, per_device(): lax.all_to_all(spectra, 'panel', split_axis=1, concat_axis=2, tiled=True)  6.6 us
  transfers between devices with their start and end apart: 1, of which 1 were waited for; matrix products, arithmetic and copies ran while one was open for 1% of the time, Pallas kernels for 0%

commit v1 on v0

v1 whole, which is shorter than its diff:
```python
import math

import jax
import jax.numpy as jnp
import numpy as np
from jax import lax
from jax.sharding import PartitionSpec as P

NS = 640
NT = 1024
NF = 96
FLO = 8
TAPS = 64
SPAN = 7
RWIN = 40
NWIN = 16
BOTH = ("freq", "panel")


def waves(freq_bins, samples):
    phases = np.outer(freq_bins, samples) % NT
    angles = phases.astype(np.float64) * (2.0 * math.pi / NT)
    return np.cos(angles), np.sin(angles)


def complex_product(left, right):
    def product(a, b):
        return jnp.dot(a, b, preferred_element_type=jnp.float32)

    real = product(left[0], right[0]) - product(left[1], right[1])
    imag = product(left[0], right[1]) + product(left[1], right[0])
    return jnp.stack([real, imag])


def solution(mesh):
    n_freq, n_panel = mesh.shape["freq"], mesh.shape["panel"]
    n_all = n_freq * n_panel
    bins = FLO + np.arange(NF)
    cosine, sine = waves(bins, np.arange(NT))
    table = np.stack([cosine, -sine], 1).reshape(2 * NF, NT)
    forward = (table / math.sqrt(NT)).astype(np.float32)
    inverse = table.astype(np.float32)
    tap_cos, tap_sin = waves(FLO + np.minimum(np.arange(n_all), NF - 1), np.arange(TAPS))
    taps = np.stack([tap_cos, -tap_sin], 1).astype(np.float32)
    rim = SPAN // 2

    def per_device(traces, filters):
        rows, cols, _ = traces.shape
        root = jnp.float32(math.sqrt(NS))
        flat = traces.reshape(rows * cols, NT)
        spectra = lax.dot_general(
            jnp.asarray(forward, jnp.bfloat16), flat, (((1,), (1,)), ((), ())),
            preferred_element_type=jnp.float32,
        ).astype(jnp.bfloat16)
        spectra = spectra.reshape(NF, 2, rows * cols)
        spectra = jnp.pad(spectra, ((0, n_all - NF), (0, 0), (0, 0)))
        slices = lax.all_to_all(spectra, BOTH, split_axis=0, concat_axis=0, tiled=True)
        slices = slices.reshape(n_freq, n_panel, 2, rows, cols)
        data = slices.transpose(2, 1, 3, 0, 4).reshape(2, NS, n_freq * cols)
        order_one = (complex_product(data, data) / root).astype(jnp.bfloat16)
        order_two = complex_product(data, order_one) / root
        prediction = (order_one.astype(jnp.float32) - order_two).astype(jnp.bfloat16)
        extended = jnp.pad(prediction, ((0, 0), (rim, rim), (0, 0))).astype(jnp.float32)
        me = lax.axis_index(BOTH)
        wave = lax.dynamic_index_in_dim(jnp.asarray(taps), me, 0, keepdims=False)
        reply = jnp.einsum("ck,wjk->cjw", wave, filters, precision=lax.Precision.HIGHEST)
        reply = jnp.repeat(reply, RWIN, axis=2)
        real = jnp.zeros((NS, n_freq * cols), jnp.float32)
        imag = real
        for j in range(SPAN):
            p_real, p_imag = extended[0, j : j + NS], extended[1, j : j + NS]
            real = real + reply[0, j] * p_real - reply[1, j] * p_imag
            imag = imag + reply[0, j] * p_imag + reply[1, j] * p_real
        matched = jnp.stack([real, imag]).astype(jnp.bfloat16)
        blocks = matched.reshape(2, n_panel, rows, n_freq, cols).transpose(3, 1, 0, 2, 4)
        blocks = blocks.reshape(n_all, 2, rows * cols)
        back = lax.all_to_all(blocks, BOTH, split_axis=0, concat_axis=0, tiled=True)
        back = back[:NF].reshape(2 * NF, rows * cols)
        multiples = lax.dot_general(
            back, jnp.asarray(inverse, jnp.bfloat16), (((0,), (0,)), ((), ())),
            preferred_element_type=jnp.float32,
        )
        multiples = multiples.reshape(rows, cols, NT) / jnp.float32(math.sqrt(NF))
        return (traces.astype(jnp.float32) - multiples).astype(jnp.bfloat16)

    placed = (P("panel", "freq", None), P())
    return jax.shard_map(
        per_device, mesh=mesh, in_specs=placed, out_specs=P("panel", "freq", None), check_vma=False
    )
```

time: 314 us -> 122 us (0.39)
  waiting for transfers between devices: 119 us -> 23.8 us
  local copies, waits for them, and re-layouts: 78.6 us -> 27.9 us
  blocking collectives: 63.2 us -> 29.7 us
  between operations: 13.7 us -> 0.28 us
  starting transfers between devices: 0.01 us -> 11.5 us
  other arithmetic: 13.1 us -> 7.67 us
  matrix products: 25 us -> 21.2 us
    all_gather x1 -> x0, waiting for transfers between devices: 119 us -> none  [per_device(): complete = lax.all_gather(columns, 'freq', axis=3, tiled=True)]
    unnamed x36 -> x10, local copies, waits for them, and re-layouts: 42.4 us -> 1.45 us
    all_to_all x2 -> x1, blocking collectives: 63.2 us -> 29.7 us  [per_device(): back = lax.all_to_all(blocks, BOTH, split_axis=0, concat_axis=0, tiled=True)]
    all_to_all x0 -> x1, waiting for transfers between devices: none -> 23.8 us  [per_device(): lax.all_to_all(spectra, BOTH, split_axis=0, concat_axis=0, tiled=True)]
    slice x5, local copies, waits for them, and re-layouts: 21.3 us -> 4.14 us  [the longest x3 3.21 us: complex_product(): real = product(left[0], right[0]) - product(left[1], right[1])]
    all_to_all x0 -> x1, starting transfers between devices: none -> 11.5 us  [per_device(): lax.all_to_all(spectra, BOTH, split_axis=0, concat_axis=0, tiled=True)]
    reshape x4 -> x6, local copies, waits for them, and re-layouts: 4.64 us -> 11.3 us  [the longest x2 6.04 us: per_device(): blocks = blocks.reshape(n_all, 2, rows * cols)]
    all_to_all x5 -> x1, local copies, waits for them, and re-layouts: 7.29 us -> 1.33 us  [per_device(): lax.all_to_all(spectra, BOTH, split_axis=0, concat_axis=0, tiled=True)]
where the time goes in v1:
time: 122 us
  blocking collectives  29.7 us (24%)
  local copies, waits for them, and re-layouts  27.9 us (23%)
  waiting for transfers between devices  23.8 us (20%)
  matrix products  21.2 us (17%)
  starting transfers between devices  11.5 us (9%)
  other arithmetic  7.67 us (6%)
    all_to_all x1, blocking collectives, per_device(): back = lax.all_to_all(blocks, BOTH, split_axis=0, concat_axis=0, tiled=True)  29.7 us
    all_to_all x1, waiting for transfers between devices, per_device(): lax.all_to_all(spectra, BOTH, split_axis=0, concat_axis=0, tiled=True)  23.8 us
    all_to_all x1, starting transfers between devices, per_device(): lax.all_to_all(spectra, BOTH, split_axis=0, concat_axis=0, tiled=True)  11.5 us
    dot_general x1, matrix products, per_device(): lax.dot_general(back, jnp.asarray(inverse, jnp.bfloat16), (((0,), (0,)),...  7.65 us
    dot_general x8, matrix products, product(): return jnp.dot(a, b, preferred_element_type=jnp.float32)  7.13 us
    reshape x2, local copies, waits for them, and re-layouts, per_device(): blocks = blocks.reshape(n_all, 2, rows * cols)  6.04 us
    another operation x2, other arithmetic  5.79 us
    dot_general x1, matrix products, per_device(): lax.dot_general(jnp.asarray(forward, jnp.bfloat16), flat, (((1,), (1,)),...  5.3 us
  transfers between devices with their start and end apart: 1, of which 1 were waited for; matrix products, arithmetic and copies ran while one was open for 1% of the time, Pallas kernels for 0%

profile of v1, /device:TPU:1, one launch (start us, length us, event | category | flops | bytes accessed | tf_op | source)
XLA Modules:
  0.0 122.0 jit_solution(3785867658899175351)
XLA Ops:
  0.0 0.0 copy-start
  0.0 5.3 %convolution_convert_fusion = bf16[192,3200]{1,0:T(8,128)(2,1)S(1)} fusion(bf16[192,1024]{1,0:T(8,128)(2,1)} %constant.33.clone, bf16[3200,1024]{1,0:T(8,128)(2,1)} %bitcast.61), kind=kOutput, calls=%fused_computation.1 | convolution fusion | flops 1258905600 | bytes 8175616 | tf_op jit(solution)/shard_map/dot_general | solution.py:51
  5.3 0.5 reshape.214
  5.8 2.3 %pad.8 = bf16[128,2,3200]{2,1,0:T(2,128)(2,1)} pad(bf16[96,2,3200]{2,1,0:T(2,128)(2,1)S(1)} %reshape.214, bf16[]{:T(256)} %constant.30.clone.1), padding=0_32x0_0x0_0 | pad | bytes 2867202 | tf_op jit(solution)/shard_map/jit(_pad)/pad | solution.py:56
  8.2 11.5 %all-to-all-start = ((bf16[128,2,3200]{2,1,0:T(2,128)(2,1)}), bf16[128,2,3200]{2,1,0:T(2,128)(2,1)S(1)}, u32[]{:S(2)}, u32[]{:S(2)}) async-start(bf16[128,2,3200]{2,1,0:T(2,128)(2,1)} %pad.8), calls=%async_computation | async-start | bytes 3276800 | tf_op jit(solution)/shard_map/all_to_all | solution.py:57
  19.7 1.1 convolution_bitcast_fusion
  20.8 0.1 broadcast_in_dim.3
  20.9 0.1 reshape.212
  21.1 0.1 slice_reduce_fusion.13
  21.2 23.8 %all-to-all-done = bf16[128,2,3200]{2,1,0:T(2,128)(2,1)S(1)} async-done(((bf16[128,2,3200]{2,1,0:T(2,128)(2,1)}), bf16[128,2,3200]{2,1,0:T(2,128)(2,1)S(1)}, u32[]{:S(2)}, u32[]{:S(2)}) %all-to-all-start) | async-done | bytes 1638432 | tf_op jit(solution)/shard_map/all_to_all | solution.py:57
  44.9 1.3 %copy.18 = bf16[128,2,3200]{2,0,1:T(8,128)(2,1)} copy(bf16[128,2,3200]{2,1,0:T(2,128)(2,1)S(1)} %all-to-all-done) | data formatting | bytes 3276800 | tf_op jit(solution)/shard_map/all_to_all | solution.py:57
  46.3 4.1 %reshape.215 = bf16[8,16,2,40,80]{4,3,1,0,2:T(8,128)(2,1)S(1)} reshape(bf16[128,2,3200]{2,0,1:T(8,128)(2,1)} %copy.18) | data formatting | bytes 3276800 | tf_op jit(solution)/shard_map/reshape | solution.py:58
  50.4 1.5 %fusion.8 = (bf16[1,16,40,8,80]{4,2,1,3,0:T(8,128)(2,1)}, bf16[1,16,40,8,80]{4,2,1,3,0:T(8,128)(2,1)S(1)}) fusion(bf16[2,16,40,8,80]{4,2,1,3,0:T(8,128)(2,1)S(1)} %bitcast.60), kind=kLoop, calls=%fused_computation.37 | loop fusion | bytes 3276800 | tf_op jit(solution)/shard_map/slice | solution.py:30
  51.9 0.8 copy.19
  52.7 0.0 copy-start.2
  52.8 1.0 squeeze.12
  53.8 0.3 copy-done.2
  54.1 0.8 copy.20
  54.9 1.0 squeeze.13
  55.9 0.9 fusion.9
  56.8 0.9 fusion.10
  57.7 0.9 add_bitcast_fusion.1
  58.6 0.9 subtract_bitcast_fusion.1
  59.5 0.3 fusion
  59.8 0.9 fusion.3
  60.7 0.9 fusion.4
  61.6 0.9 subtract_bitcast_fusion
  62.5 0.9 add_bitcast_fusion
  63.5 0.6 fusion.2
  64.1 0.3 pad_convert_fusion
  64.4 3.0 %subtract_convert_fusion.1 = bf16[1,640,640]{2,1,0:T(8,128)(2,1)S(1)} fusion(f32[2,646,640]{2,1,0:T(8,128)S(1)} %pad_convert_fusion, f32[640]{0:T(1024)S(1)} %get-tuple-element.6, f32[640]{0:T(1024)S(1)} %get-tuple-element.7, f32[640]{0:T(1024)S(1)} %get-tuple-element.8, f32[640]{0:T(1024)S(1)} %get-tuple-element.9, f32[640]{0:T(1024)S(1)} %get-tuple-element.10, ...), kind=kLoop, calls=%fused_computation.10 | loop fusion | flops 11468800 | bytes 23792640 | tf_op jit(solution)/shard_map/convert.3
  67.4 2.8 %add_convert_fusion = bf16[1,640,640]{2,1,0:T(8,128)(2,1)S(1)} fusion(f32[2,646,640]{2,1,0:T(8,128)S(1)} %pad_convert_fusion, f32[640]{0:T(1024)S(1)} %get-tuple-element.6, f32[640]{0:T(1024)S(1)} %get-tuple-element.7, f32[640]{0:T(1024)S(1)} %get-tuple-element.8, f32[640]{0:T(1024)S(1)} %get-tuple-element.9, f32[640]{0:T(1024)S(1)} %get-tuple-element.10, ...), kind=kLoop, calls=%fused_computation.9 | loop fusion | flops 11468800 | bytes 23792640 | tf_op jit(solution)/shard_map/convert.2
  70.2 1.4 %stack.33 = bf16[1,16,40,8,80]{4,3,2,1,0:T(8,128)(2,1)S(1)} reshape(bf16[1,640,640]{2,1,0:T(8,128)(2,1)S(1)} %subtract_convert_fusion.1) | data formatting | bytes 1638400 | tf_op jit(solution)/shard_map/stack | solution.py:74
  71.6 1.3 %copy.21 = bf16[1,16,40,8,80]{4,2,1,3,0:T(8,128)(2,1)} copy(bf16[1,16,40,8,80]{4,3,2,1,0:T(8,128)(2,1)S(1)} %stack.33) | data formatting | bytes 1638400 | tf_op jit(solution)/shard_map/stack | solution.py:74
  72.9 1.4 %stack.34 = bf16[1,16,40,8,80]{4,3,2,1,0:T(8,128)(2,1)S(1)} reshape(bf16[1,640,640]{2,1,0:T(8,128)(2,1)S(1)} %add_convert_fusion) | data formatting | bytes 1638400 | tf_op jit(solution)/shard_map/stack | solution.py:74
  74.3 0.0 copy-start.3
  74.3 0.2 copy.22
  74.4 1.1 copy-done.3
  75.6 0.6 maximum_bitcast_fusion
  76.2 2.9 %reshape.216 = bf16[128,2,3200]{2,0,1:T(8,128)(2,1)} reshape(bf16[8,16,2,40,80]{4,3,1,0,2:T(8,128)(2,1)S(1)} %maximum_bitcast_fusion) | data formatting | bytes 3276800 | tf_op jit(solution)/shard_map/reshape | solution.py:76
  79.1 3.1 %copy.23 = bf16[128,2,3200]{2,1,0:T(2,128)(2,1)S(1)} copy(bf16[128,2,3200]{2,0,1:T(8,128)(2,1)} %reshape.216) | data formatting | bytes 3276800 | tf_op jit(solution)/shard_map/reshape | solution.py:76
  82.2 29.7 %all_to_all.10 = bf16[128,2,3200]{2,1,0:T(2,128)(2,1)S(1)} all-to-all(bf16[128,2,3200]{2,1,0:T(2,128)(2,1)S(1)} %copy.23), channel_id=1, replica_groups=mesh['freq'=8,'panel'=16] {'freq','panel'}, dimensions={0} | all-to-all | bytes 3276800 | tf_op jit(solution)/shard_map/all_to_all | solution.py:77
  111.9 0.8 slice.192
  112.8 0.5 reshape.217
  113.3 0.0 copy-start.4
  113.3 1.0 copy.24
  114.3 0.0 copy-start.1
  114.4 7.7 %subtract_convert_fusion = bf16[40,80,1024]{2,1,0:T(8,128)(2,1)} fusion(bf16[40,80,1024]{2,1,0:T(8,128)(2,1)} %param.5, bf16[40,80,192]{2,1,0:T(8,128)(2,1)S(1)} %bitcast.63, bf16[192,1024,1]{1,0,2:T(8,128)(2,1)S(1)} %copy-done.4), kind=kOutput, calls=%fused_computation | convolution fusion | flops 1271398400 | bytes 14729216 | tf_op jit(solution)/shard_map/dot_general | solution.py:79
  (3 shorter events, 0.0 us)
Async XLA Ops:
  0.0 19.7 %copy-start = (f32[16,7,64]{2,0,1:T(8,128)S(1)}, f32[16,7,64]{2,0,1:T(8,128)}, u32[]{:S(2)}) copy-start(f32[16,7,64]{2,0,1:T(8,128)} %param.6) | copy-start | bytes 86020
  8.2 36.8 %all-to-all-start = ((bf16[128,2,3200]{2,1,0:T(2,128)(2,1)}), bf16[128,2,3200]{2,1,0:T(2,128)(2,1)S(1)}, u32[]{:S(2)}, u32[]{:S(2)}) async-start(bf16[128,2,3200]{2,1,0:T(2,128)(2,1)} %pad.8), calls=%async_computation | async-start | bytes 3276800 | tf_op jit(solution)/shard_map/all_to_all | solution.py:57
  52.7 1.3 %copy-start.2 = (bf16[1,16,40,8,80]{4,2,1,3,0:T(8,128)(2,1)S(1)}, bf16[1,16,40,8,80]{4,2,1,3,0:T(8,128)(2,1)}, u32[]{:S(2)}) copy-start(bf16[1,16,40,8,80]{4,2,1,3,0:T(8,128)(2,1)} %get-tuple-element.19) | copy-start | bytes 2457604
  74.3 1.3 %copy-start.3 = (bf16[1,16,40,8,80]{4,2,1,3,0:T(8,128)(2,1)S(1)}, bf16[1,16,40,8,80]{4,2,1,3,0:T(8,128)(2,1)}, u32[]{:S(2)}) copy-start(bf16[1,16,40,8,80]{4,2,1,3,0:T(8,128)(2,1)} %copy.21) | copy-start | bytes 2457604
  113.3 1.0 copy-start.4
  114.3 7.7 %copy-start.1 = (f32[16,7,64]{2,0,1:T(8,128)S(1)}, f32[16,7,64]{2,0,1:T(8,128)}, u32[]{:S(2)}) copy-start(f32[16,7,64]{2,0,1:T(8,128)} %param.6) | copy-start | bytes 86020

commit v2 on v1

v2 whole, which is shorter than its diff:
```python
import functools
import math

import jax
import jax.numpy as jnp
import numpy as np
from jax import lax
from jax.experimental import pallas as pl
from jax.experimental.pallas import tpu as pltpu
from jax.sharding import PartitionSpec as P

NS = 640
NT = 1024
NF = 96
FLO = 8
TAPS = 64
SPAN = 7
RWIN = 40
NWIN = 16
BOTH = ("freq", "panel")


def waves(freq_bins, samples):
    phases = np.outer(freq_bins, samples) % NT
    angles = phases.astype(np.float64) * (2.0 * math.pi / NT)
    return np.cos(angles), np.sin(angles)


def mid_kernel(x_ref, w_ref, y_ref, z_ref, l_ref, r_ref, o_ref, f_ref, *, n_freq, n_panel, rows, cols):
    f32, bf16 = jnp.float32, jnp.bfloat16
    pair = 2 * n_panel
    width = n_freq * cols
    tiles = width // 128
    group = width // cols
    groups = rows // group
    lane = lax.broadcasted_iota(jnp.int32, (pair, 128), 1)
    root = 1.0 / math.sqrt(NS)

    def gather(read, outer, t):
        value = None
        for piece in range(group):
            lo, hi = max(piece * cols, t * 128), min((piece + 1) * cols, t * 128 + 128)
            if lo >= hi:
                continue
            src_lo = outer * cols + lo - piece * cols
            src_hi = src_lo + hi - lo
            for tile in range(src_lo // 128, (src_hi - 1) // 128 + 1):
                a, b = max(src_lo, tile * 128), min(src_hi, tile * 128 + 128)
                d0, d1 = a - src_lo + lo - t * 128, b - src_lo + lo - t * 128
                shift = (d0 - (a - tile * 128)) % 128
                v = read(piece, tile)
                if shift:
                    v = pltpu.roll(v, shift, 1)
                value = v if value is None else jnp.where((lane >= d0) & (lane < d1), v, value)
        return value

    def split(g, _):
        base = pl.multiple_of(g * width, 128)
        for s in range(group):
            def read(q, tile):
                return x_ref[q * pair:(q + 1) * pair, pl.ds(pl.multiple_of(base + tile * 128, 128), 128)].astype(f32)
            for t in range(tiles):
                z_ref[t, pl.ds(g * group + s, pair, stride=rows), :] = gather(read, s, t)
        return 0
    lax.fori_loop(0, groups, split, 0)

    def place(p, _):
        row = pl.multiple_of(p * 2 * rows, 16)
        for t in range(tiles):
            z = z_ref[t, pl.ds(pl.multiple_of(p * 4 * rows, 8), 4 * rows), :]
            re = jnp.concatenate([z[:rows], z[2 * rows:3 * rows]], 0)
            im = jnp.concatenate([z[rows:2 * rows], z[3 * rows:]], 0)
            c = slice(t * 128, t * 128 + 128); d = slice(width + t * 128, width + t * 128 + 128)
            reb, imb = re.astype(bf16), im.astype(bf16)
            l_ref[pl.ds(row, 2 * rows), c] = reb
            l_ref[pl.ds(row, 2 * rows), d] = imb
            r_ref[pl.ds(row, 2 * rows), c] = reb
            r_ref[pl.ds(row, 2 * rows), d] = imb
            r_ref[pl.ds(row + NS, 2 * rows), c] = (-im).astype(bf16)
            r_ref[pl.ds(row + NS, 2 * rows), d] = reb
        return 0
    lax.fori_loop(0, n_panel // 2, place, 0)

    step = 256
    for n in range(2 * width // step):
        c = slice(n * step, n * step + step)
        o = jnp.dot(l_ref[...], r_ref[:, c], preferred_element_type=f32) * root
        for h in range(step // 128):
            t = n * (step // 128) + h
            ob = o[:, h * 128:h * 128 + 128]
            o_ref[:NS, t * 128:t * 128 + 128] = ob.astype(bf16)
            if t < tiles:
                o_ref[NS:, width + t * 128:width + t * 128 + 128] = ob.astype(bf16)
            else:
                o_ref[NS:, (t - tiles) * 128:(t - tiles) * 128 + 128] = (-ob).astype(bf16)
    zero = jnp.zeros((8, 128), f32)
    for t in range(2 * tiles):
        f_ref[t, 0:8, :] = zero
        f_ref[t, 8 + NS:16 + NS, :] = zero
    for n in range(2 * width // step):
        c = slice(n * step, n * step + step)
        o = jnp.dot(l_ref[...], o_ref[:, c], preferred_element_type=f32) * root
        pred = (o_ref[:NS, c].astype(f32) - o).astype(bf16).astype(f32)
        for h in range(step // 128):
            f_ref[n * (step // 128) + h, 8:8 + NS, :] = pred[:, h * 128:h * 128 + 128]

    rim = SPAN // 2
    for t in range(tiles):
        weights = [jnp.broadcast_to(w_ref[i:i + 1, t * 128:t * 128 + 128], (rows, 128)) for i in range(2 * SPAN)]
        def match(p, _):
            real = imag = None
            for j in range(SPAN):
                at = pl.ds(p * rows + 8 - rim + j, rows)
                a, b = f_ref[t, at, :], f_ref[tiles + t, at, :]
                wr, wi = weights[j], weights[SPAN + j]
                re, im = wr * a - wi * b, wr * b + wi * a
                real, imag = (re, im) if real is None else (real + re, imag + im)
            z_ref[t, pl.ds(pl.multiple_of(p * 2 * rows, 8), rows), :] = real
            z_ref[t, pl.ds(pl.multiple_of(p * 2 * rows + rows, 8), rows), :] = imag
            return 0
        lax.fori_loop(0, n_panel, match, 0)

    def join(g, _):
        base = pl.multiple_of(g * width, 128)
        def read(s, tile):
            return z_ref[tile, pl.ds(g * group + s, pair, stride=rows), :]
        for q in range(n_freq):
            for t in range(tiles):
                y_ref[q * pair:(q + 1) * pair, pl.ds(pl.multiple_of(base + t * 128, 128), 128)] = gather(read, q, t).astype(bf16)
        return 0
    lax.fori_loop(0, groups, join, 0)


def middle(x, w, n_freq, n_panel, rows, cols):
    width = n_freq * cols
    f32, bf16 = jnp.float32, jnp.bfloat16
    return pl.pallas_call(
        functools.partial(mid_kernel, n_freq=n_freq, n_panel=n_panel, rows=rows, cols=cols),
        out_shape=jax.ShapeDtypeStruct(x.shape, bf16),
        scratch_shapes=[
            pltpu.VMEM((width // 128, 2 * NS, 128), f32),
            pltpu.VMEM((NS, 2 * width), bf16),
            pltpu.VMEM((2 * NS, 2 * width), bf16),
            pltpu.VMEM((2 * NS, 2 * width), bf16),
            pltpu.VMEM((2 * width // 128, NS + 16, 128), f32),
        ],
        compiler_params=pltpu.CompilerParams(vmem_limit_bytes=56 << 20),
    )(x, w)


def solution(mesh):
    n_freq, n_panel = mesh.shape["freq"], mesh.shape["panel"]
    n_all = n_freq * n_panel
    bins = FLO + np.arange(NF)
    cosine, sine = waves(bins, np.arange(NT))
    table = np.stack([cosine, -sine], 1).reshape(2 * NF, NT)
    forward = np.pad(table / math.sqrt(NT), ((0, 2 * (n_all - NF)), (0, 0))).astype(np.float32)
    inverse = table.astype(np.float32)
    tap_cos, tap_sin = waves(FLO + np.minimum(np.arange(n_all), NF - 1), np.arange(TAPS))
    taps = np.stack([tap_cos, -tap_sin], 1).astype(np.float32)

    def per_device(traces, filters):
        rows, cols, _ = traces.shape
        flat = traces.reshape(rows * cols, NT)
        spectra = lax.dot_general(
            jnp.asarray(forward, jnp.bfloat16), flat, (((1,), (1,)), ((), ())),
            preferred_element_type=jnp.float32,
        ).astype(jnp.bfloat16)
        spectra = spectra.reshape(n_all, 2, rows * cols)
        slices = lax.all_to_all(spectra, BOTH, split_axis=0, concat_axis=0, tiled=True)
        me = lax.axis_index(BOTH)
        wave = lax.dynamic_index_in_dim(jnp.asarray(taps), me, 0, keepdims=False)
        reply = jnp.einsum("ck,wjk->cjw", wave, filters, precision=lax.Precision.HIGHEST)
        reply = jnp.repeat(reply, RWIN, axis=2).reshape(2 * SPAN, n_freq * cols)
        matched = middle(
            slices.reshape(2 * n_all, rows * cols), reply, n_freq, n_panel, rows, cols
        ).reshape(n_all, 2, rows * cols)
        back = lax.all_to_all(matched, BOTH, split_axis=0, concat_axis=0, tiled=True)
        back = back[:NF].reshape(2 * NF, rows * cols)
        multiples = lax.dot_general(
            back, jnp.asarray(inverse, jnp.bfloat16), (((0,), (0,)), ((), ())),
            preferred_element_type=jnp.float32,
        )
        multiples = multiples.reshape(rows, cols, NT) / jnp.float32(math.sqrt(NF))
        return (traces.astype(jnp.float32) - multiples).astype(jnp.bfloat16)

    placed = (P("panel", "freq", None), P())
    return jax.shard_map(
        per_device, mesh=mesh, in_specs=placed, out_specs=P("panel", "freq", None), check_vma=False
    )
```

time: 122 us -> 104 us (0.85)
  local copies, waits for them, and re-layouts: 27.9 us -> 10.5 us
  Pallas kernels: 0 us -> 14.6 us
  other arithmetic: 7.67 us -> 0 us
  matrix products: 21.2 us -> 14.2 us
    pallas_call x0 -> x1, Pallas kernels: none -> 14.6 us  [middle(): pl.pallas_call(functools.partial(mid_kernel, n_freq=n_freq, n_panel=n_pan...]
    dot_general x8 -> x0, matrix products: 7.13 us -> none  [product(): return jnp.dot(a, b, preferred_element_type=jnp.float32)]
    another operation x2 -> x0, other arithmetic: 5.79 us -> none
    reshape x5 -> x3, local copies, waits for them, and re-layouts: 10.8 us -> 6.63 us  [the longest x1 3.57 us: per_device(): matched = middle(slices.reshape(2 * n_all, rows * cols), reply, n_freq, n...]
    another operation x4 -> x1, local copies, waits for them, and re-layouts: 4.19 us -> 0.73 us  [per_device(): reply = jnp.repeat(reply, RWIN, axis=2).reshape(2 * SPAN, n_freq * cols)]
    slice x4 -> x0, local copies, waits for them, and re-layouts: 3.3 us -> none  [the longest x3 3.21 us: complex_product(): real = product(left[0], right[0]) - product(left[1], right[1])]
    pad x1 -> x0, local copies, waits for them, and re-layouts: 2.32 us -> none  [per_device(): spectra = jnp.pad(spectra, ((0, n_all - NF), (0, 0), (0, 0)))]
    squeeze x2 -> x0, local copies, waits for them, and re-layouts: 2.01 us -> none  [complex_product(): real = product(left[0], right[0]) - product(left[1], right[1])]
  transfers between devices with their start and end apart: 1 -> 1, of which waited for: 1 -> 1; matrix products, arithmetic and copies ran while one was open for 1% -> 2% of each run, Pallas kernels for 0% -> 0%
where the time goes in v2:
time: 104 us
  blocking collectives  29.7 us (29%)
  waiting for transfers between devices  23.3 us (22%)
  Pallas kernels  14.6 us (14%)
  matrix products  14.2 us (14%)
  starting transfers between devices  11.5 us (11%)
  local copies, waits for them, and re-layouts  10.5 us (10%)
    all_to_all x1, blocking collectives, per_device(): lax.all_to_all(matched, BOTH, split_axis=0, concat_axis=0, tiled=True)  29.7 us
    all_to_all x1, waiting for transfers between devices, per_device(): lax.all_to_all(spectra, BOTH, split_axis=0, concat_axis=0, tiled=True)  23.3 us
    pallas_call x1, Pallas kernels, middle(): pl.pallas_call(functools.partial(mid_kernel, n_freq=n_freq, n_panel=n_pan...  14.6 us
    all_to_all x1, starting transfers between devices, per_device(): lax.all_to_all(spectra, BOTH, split_axis=0, concat_axis=0, tiled=True)  11.5 us
    dot_general x1, matrix products, per_device(): lax.dot_general(back, jnp.asarray(inverse, jnp.bfloat16), (((0,), (0,)),...  8.02 us
    dot_general x1, matrix products, per_device(): lax.dot_general(jnp.asarray(forward, jnp.bfloat16), flat, (((1,), (1,)),...  5.02 us
    reshape x1, local copies, waits for them, and re-layouts, per_device(): matched = middle(slices.reshape(2 * n_all, rows * cols), reply, n_freq, n...  3.57 us
    reshape x2, local copies, waits for them, and re-layouts, per_device(): back = back[:NF].reshape(2 * NF, rows * cols)  2.22 us
  transfers between devices with their start and end apart: 1, of which 1 were waited for; matrix products, arithmetic and copies ran while one was open for 2% of the time, Pallas kernels for 0%

profile of v2, /device:TPU:1, one launch (start us, length us, event | category | flops | bytes accessed | tf_op | source)
XLA Modules:
  0.0 103.9 jit_solution(9354054658111113315)
XLA Ops:
  0.0 0.0 copy-start
  0.0 5.0 %convolution_convert_fusion = bf16[256,3200]{1,0:T(8,128)(2,1)S(1)} fusion(bf16[256,1024]{1,0:T(8,128)(2,1)} %constant.26.clone, bf16[3200,1024]{1,0:T(8,128)(2,1)} %bitcast.19), kind=kOutput, calls=%fused_computation.1 | convolution fusion | flops 1678540800 | bytes 8716288 | tf_op jit(solution)/shard_map/dot_general | solution.py:165
  5.0 1.5 %reshape.18 = bf16[128,2,3200]{2,1,0:T(2,128)(2,1)} reshape(bf16[256,3200]{1,0:T(8,128)(2,1)S(1)} %convolution_convert_fusion) | data formatting | bytes 3276800 | tf_op jit(solution)/shard_map/reshape | solution.py:169
  6.6 11.5 %all-to-all-start = ((bf16[128,2,3200]{2,1,0:T(2,128)(2,1)}), bf16[128,2,3200]{2,1,0:T(2,128)(2,1)S(1)}, u32[]{:S(2)}, u32[]{:S(2)}) async-start(bf16[128,2,3200]{2,1,0:T(2,128)(2,1)} %reshape.18), calls=%async_computation | async-start | bytes 3276800 | tf_op jit(solution)/shard_map/all_to_all | solution.py:170
  18.1 0.0 copy-done
  18.1 1.1 %convolution_bitcast_fusion = f32[2,7,16]{2,0,1:T(2,128)S(1)} fusion(f32[16,7,64]{2,0,1:T(8,128)S(1)} %copy-done, f32[128,2,64]{2,1,0:T(2,128)} %constant.27.clone, s32[]{:T(128)S(6)} %select_n.4), kind=kOutput, calls=%fused_computation.2 | convolution fusion | flops 172032 | bytes 30596 | tf_op jit(solution)/shard_map/ck,wjk->cjw/dot_general | solution.py:173
  19.2 0.1 broadcast_in_dim.3
  19.3 0.7 reshape_reshape.3.w_ref
  20.1 23.3 %all-to-all-done = bf16[128,2,3200]{2,1,0:T(2,128)(2,1)S(1)} async-done(((bf16[128,2,3200]{2,1,0:T(2,128)(2,1)}), bf16[128,2,3200]{2,1,0:T(2,128)(2,1)S(1)}, u32[]{:S(2)}, u32[]{:S(2)}) %all-to-all-start) | async-done | bytes 1638432 | tf_op jit(solution)/shard_map/all_to_all | solution.py:170
  43.3 1.5 %reshape.19.x_ref = bf16[256,3200]{1,0:T(8,128)(2,1)} reshape(bf16[128,2,3200]{2,1,0:T(2,128)(2,1)S(1)} %all-to-all-done) | data formatting | bytes 3276800 | tf_op jit(solution)/shard_map/reshape | solution.py:176
  44.9 14.6 %shard_map.55 = bf16[256,3200]{1,0:T(8,128)(2,1)} custom-call(bf16[256,3200]{1,0:T(8,128)(2,1)} %reshape.19.x_ref, f32[14,640]{1,0:T(8,128)} %reshape_reshape.3.w_ref), custom_call_target="tpu_custom_call" | custom-call | tf_op jit(solution)/shard_map/pallas_call | solution.py:137
  59.5 3.6 %reshape.20 = bf16[128,2,3200]{2,1,0:T(2,128)(2,1)S(1)} reshape(bf16[256,3200]{1,0:T(8,128)(2,1)} %shard_map.55) | data formatting | bytes 3276800 | tf_op jit(solution)/shard_map/reshape | solution.py:177
  63.0 29.7 %all_to_all.10 = bf16[128,2,3200]{2,1,0:T(2,128)(2,1)S(1)} all-to-all(bf16[128,2,3200]{2,1,0:T(2,128)(2,1)S(1)} %reshape.20), channel_id=1, replica_groups=mesh['freq'=8,'panel'=16] {'freq','panel'}, dimensions={0} | all-to-all | bytes 3276800 | tf_op jit(solution)/shard_map/all_to_all | solution.py:178
  92.8 0.8 slice.4
  93.6 0.5 reshape.21
  94.1 0.0 copy-start.1
  94.1 1.7 %copy.7 = bf16[192,3200]{0,1:T(8,128)(2,1)} copy(bf16[192,3200]{1,0:T(8,128)(2,1)S(1)} %reshape.21) | data formatting | bytes 2457600 | tf_op jit(solution)/shard_map/reshape | solution.py:179
  95.8 0.0 copy-done.1
  95.8 8.0 %subtract_convert_fusion = bf16[40,80,1024]{2,1,0:T(8,128)(2,1)} fusion(bf16[40,80,1024]{2,1,0:T(8,128)(2,1)} %param.5, bf16[40,80,192]{2,1,0:T(8,128)(2,1)} %bitcast.18, bf16[192,1024,1]{1,0,2:T(8,128)(2,1)S(1)} %copy-done.1), kind=kOutput, calls=%fused_computation | convolution fusion | flops 1271398400 | bytes 14729216 | tf_op jit(solution)/shard_map/dot_general | solution.py:180
  (1 shorter events, 0.0 us)
Async XLA Ops:
  0.0 18.1 %copy-start = (f32[16,7,64]{2,0,1:T(8,128)S(1)}, f32[16,7,64]{2,0,1:T(8,128)}, u32[]{:S(2)}) copy-start(f32[16,7,64]{2,0,1:T(8,128)} %param.6) | copy-start | bytes 86020
  6.6 36.8 %all-to-all-start = ((bf16[128,2,3200]{2,1,0:T(2,128)(2,1)}), bf16[128,2,3200]{2,1,0:T(2,128)(2,1)S(1)}, u32[]{:S(2)}, u32[]{:S(2)}) async-start(bf16[128,2,3200]{2,1,0:T(2,128)(2,1)} %reshape.18), calls=%async_computation | async-start | bytes 3276800 | tf_op jit(solution)/shard_map/all_to_all | solution.py:170
  94.1 1.7 %copy-start.1 = (bf16[192,1024,1]{1,0,2:T(8,128)(2,1)S(1)}, bf16[192,1024,1]{1,0,2:T(8,128)(2,1)}, u32[]{:S(2)}) copy-start(bf16[192,1024,1]{1,0,2:T(8,128)(2,1)} %constant.30) | copy-start | bytes 1179652

commit v3 on v2

--- a/solution.py
+++ b/solution.py
@@ -136,7 +136,9 @@
     f32, bf16 = jnp.float32, jnp.bfloat16
     return pl.pallas_call(
         functools.partial(mid_kernel, n_freq=n_freq, n_panel=n_panel, rows=rows, cols=cols),
-        out_shape=jax.ShapeDtypeStruct(x.shape, bf16),
+        out_shape=pltpu.VMEM(x.shape, bf16),
+        in_specs=[pl.BlockSpec(memory_space=pltpu.VMEM)] * 2,
+        out_specs=pl.BlockSpec(memory_space=pltpu.VMEM),
         scratch_shapes=[
             pltpu.VMEM((width // 128, 2 * NS, 128), f32),
             pltpu.VMEM((NS, 2 * width), bf16),
@@ -144,8 +146,95 @@
             pltpu.VMEM((2 * NS, 2 * width), bf16),
             pltpu.VMEM((2 * width // 128, NS + 16, 128), f32),
         ],
-        compiler_params=pltpu.CompilerParams(vmem_limit_bytes=56 << 20),
+        compiler_params=pltpu.CompilerParams(vmem_limit_bytes=22 << 20),
     )(x, w)
+
+
+def first_kernel(t_hbm, f_ref, s_ref, t_ref, sem, *, group):
+    rows, cols, _ = t_ref.shape
+    width, half = group * cols, group * cols // 2
+    used = f_ref.shape[1]
+
+    def copy(g):
+        at = pl.ds(g * group, group)
+        return pltpu.make_async_copy(t_hbm.at[at], t_ref.at[at], sem.at[g])
+
+    for g in range(rows // group):
+        copy(g).start()
+    s_ref[used:, :] = jnp.zeros((s_ref.shape[0] - used, s_ref.shape[1]), s_ref.dtype)
+    for g in range(rows // group):
+        copy(g).wait()
+        block = t_ref[g * group : (g + 1) * group].reshape(width, NT)
+        out = jnp.concatenate(
+            [
+                jnp.dot(part, f_ref[...], preferred_element_type=jnp.float32)
+                for part in (block[:half], block[half:])
+            ],
+            0,
+        )
+        s_ref[:used, g * width : (g + 1) * width] = out.astype(s_ref.dtype).T
+
+
+def first(traces, forward, n_all, group=8):
+    rows, cols, _ = traces.shape
+    return pl.pallas_call(
+        functools.partial(first_kernel, group=group),
+        out_shape=pltpu.VMEM((2 * n_all, rows * cols), jnp.bfloat16),
+        in_specs=[
+            pl.BlockSpec(memory_space=pltpu.HBM),
+            pl.BlockSpec(memory_space=pltpu.VMEM),
+        ],
+        out_specs=pl.BlockSpec(memory_space=pltpu.VMEM),
+        scratch_shapes=[pltpu.VMEM(traces.shape, jnp.bfloat16), pltpu.SemaphoreType.DMA((rows // group,))],
+        compiler_params=pltpu.CompilerParams(vmem_limit_bytes=20 << 20),
+    )(pltpu.with_memory_space_constraint(traces, pltpu.HBM), forward)
+
+
+def last_kernel(m_ref, t_hbm, i_ref, o_hbm, t_ref, o_ref, t_sem, sem, *, group, part):
+    rows, cols, _ = t_ref.shape
+    width = group * cols
+    used = i_ref.shape[0]
+    scale = 1.0 / math.sqrt(NF)
+    steps = group // part
+    def copy(g, h):
+        at = pl.ds(g * group + h * part, part)
+        return pltpu.make_async_copy(o_ref.at[at], o_hbm.at[at], sem)
+    def fetch(g):
+        at = pl.ds(g * group, group)
+        return pltpu.make_async_copy(t_hbm.at[at], t_ref.at[at], t_sem.at[g])
+
+    for g in range(rows // group):
+        fetch(g).start()
+    for g in range(rows // group):
+        fetch(g).wait()
+        mt = m_ref[:used, g * width:(g + 1) * width].T
+        for h in range(steps):
+            acc = jnp.dot(mt[h * part * cols:(h + 1) * part * cols], i_ref[...], preferred_element_type=jnp.float32)
+            at = slice(g * group + h * part, g * group + (h + 1) * part)
+            t = t_ref[at].astype(jnp.float32)
+            o_ref[at] = (t - (acc * scale).reshape(t.shape)).astype(o_ref.dtype)
+            copy(g, h).start()
+    pltpu.make_async_copy(o_ref, o_hbm, sem).wait()
+
+
+def last(m, traces, inverse, group=8, part=2):
+    return pl.pallas_call(
+        functools.partial(last_kernel, group=group, part=part),
+        out_shape=jax.ShapeDtypeStruct(traces.shape, jnp.bfloat16),
+        in_specs=[
+            pl.BlockSpec(memory_space=pltpu.VMEM),
+            pl.BlockSpec(memory_space=pltpu.HBM),
+            pl.BlockSpec(memory_space=pltpu.VMEM),
+        ],
+        out_specs=pl.BlockSpec(memory_space=pltpu.HBM),
+        scratch_shapes=[
+            pltpu.VMEM(traces.shape, jnp.bfloat16),
+            pltpu.VMEM(traces.shape, jnp.bfloat16),
+            pltpu.SemaphoreType.DMA((traces.shape[0] // group,)),
+            pltpu.SemaphoreType.DMA(()),
+        ],
+        compiler_params=pltpu.CompilerParams(vmem_limit_bytes=24 << 20),
+    )(m, pltpu.with_memory_space_constraint(traces, pltpu.HBM), inverse)
 
 
 def solution(mesh):
@@ -154,18 +243,14 @@
     bins = FLO + np.arange(NF)
     cosine, sine = waves(bins, np.arange(NT))
     table = np.stack([cosine, -sine], 1).reshape(2 * NF, NT)
-    forward = np.pad(table / math.sqrt(NT), ((0, 2 * (n_all - NF)), (0, 0))).astype(np.float32)
+    forward = (table / math.sqrt(NT)).astype(np.float32).T
     inverse = table.astype(np.float32)
     tap_cos, tap_sin = waves(FLO + np.minimum(np.arange(n_all), NF - 1), np.arange(TAPS))
     taps = np.stack([tap_cos, -tap_sin], 1).astype(np.float32)
 
     def per_device(traces, filters):
         rows, cols, _ = traces.shape
-        flat = traces.reshape(rows * cols, NT)
-        spectra = lax.dot_general(
-            jnp.asarray(forward, jnp.bfloat16), flat, (((1,), (1,)), ((), ())),
-            preferred_element_type=jnp.float32,
-        ).astype(jnp.bfloat16)
+        spectra = first(traces, jnp.asarray(forward, jnp.bfloat16), n_all)
         spectra = spectra.reshape(n_all, 2, rows * cols)
         slices = lax.all_to_all(spectra, BOTH, split_axis=0, concat_axis=0, tiled=True)
         me = lax.axis_index(BOTH)
@@ -176,13 +261,8 @@
             slices.reshape(2 * n_all, rows * cols), reply, n_freq, n_panel, rows, cols
         ).reshape(n_all, 2, rows * cols)
         back = lax.all_to_all(matched, BOTH, split_axis=0, concat_axis=0, tiled=True)
-        back = back[:NF].reshape(2 * NF, rows * cols)
-        multiples = lax.dot_general(
-            back, jnp.asarray(inverse, jnp.bfloat16), (((0,), (0,)), ((), ())),
-            preferred_element_type=jnp.float32,
-        )
-        multiples = multiples.reshape(rows, cols, NT) / jnp.float32(math.sqrt(NF))
-        return (traces.astype(jnp.float32) - multiples).astype(jnp.bfloat16)
+        back = back.reshape(2 * n_all, rows * cols)
+        return last(back, traces, jnp.asarray(inverse, jnp.bfloat16))
 
     placed = (P("panel", "freq", None), P())
     return jax.shard_map(

time: 104 us -> 96.5 us (0.928)
  matrix products: 14.2 us -> 1.12 us
  Pallas kernels: 14.6 us -> 21.4 us
  local copies, waits for them, and re-layouts: 10.5 us -> 7.89 us
    dot_general x2 -> x0, matrix products: 13 us -> none  [the longest x1 8.02 us: per_device(): lax.dot_general(back, jnp.asarray(inverse, jnp.bfloat16), (((0,), (0,)),...]
    pallas_call x0 -> x2, Pallas kernels: none -> 9.42 us  [the longest x1 5.07 us: last(): pl.pallas_call(functools.partial(last_kernel, group=group, part=part), ou...]
    reshape x1, local copies, waits for them, and re-layouts: 3.57 us -> 0.66 us  [per_device(): matched = middle(slices.reshape(2 * n_all, rows * cols), reply, n_freq, n...]
    pallas_call x1, Pallas kernels: 14.6 us -> 12 us  [middle(): pl.pallas_call(functools.partial(mid_kernel, n_freq=n_freq, n_panel=n_pan...]
    reshape x2 -> x1, local copies, waits for them, and re-layouts: 2.22 us -> 3.77 us  [per_device(): back = back.reshape(2 * n_all, rows * cols)]
    unnamed x4 -> x6, local copies, waits for them, and re-layouts: 0.01 us -> 1.06 us
  transfers between devices with their start and end apart: 1 -> 1, of which waited for: 1 -> 1; matrix products, arithmetic and copies ran while one was open for 2% -> 1% of each run, Pallas kernels for 0% -> 0%
where the time goes in v3:
time: 96.5 us; the launch traced here: 96.2 us
  blocking collectives  30.1 us (31%)
  waiting for transfers between devices  23.9 us (25%)
  Pallas kernels  21.4 us (22%)
  starting transfers between devices  11.5 us (12%)
  local copies, waits for them, and re-layouts  7.89 us (8%)
  matrix products  1.12 us (1%)
    all_to_all x1, blocking collectives, per_device(): lax.all_to_all(matched, BOTH, split_axis=0, concat_axis=0, tiled=True)  30.1 us
    all_to_all x1, waiting for transfers between devices, per_device(): lax.all_to_all(spectra, BOTH, split_axis=0, concat_axis=0, tiled=True)  23.9 us
    pallas_call x1, Pallas kernels, middle(): pl.pallas_call(functools.partial(mid_kernel, n_freq=n_freq, n_panel=n_pan...  12 us
    all_to_all x1, starting transfers between devices, per_device(): lax.all_to_all(spectra, BOTH, split_axis=0, concat_axis=0, tiled=True)  11.5 us
    pallas_call x1, Pallas kernels, last(): pl.pallas_call(functools.partial(last_kernel, group=group, part=part), ou...  5.07 us
    pallas_call x1, Pallas kernels, first(): pl.pallas_call(functools.partial(first_kernel, group=group), out_shape=pl...  4.35 us
    reshape x1, local copies, waits for them, and re-layouts, per_device(): back = back.reshape(2 * n_all, rows * cols)  3.77 us
  transfers between devices with their start and end apart: 1, of which 1 were waited for; matrix products, arithmetic and copies ran while one was open for 1% of the time, Pallas kernels for 0%

profile of v3, /device:TPU:1, one launch (start us, length us, event | category | flops | bytes accessed | tf_op | source)
XLA Modules:
  0.0 96.2 jit_solution(10773244223749483447)
XLA Ops:
  0.0 0.0 copy-start
  0.0 0.0 copy-start.1
  0.0 1.0 %copy-done.1 = bf16[1024,192]{1,0:T(8,128)(2,1)S(1)} copy-done((bf16[1024,192]{1,0:T(8,128)(2,1)S(1)}, bf16[1024,192]{1,0:T(8,128)(2,1)}, u32[]{:S(2)}) %copy-start.1) | copy-done | bytes 393240
  1.1 4.3 %shard_map.55 = bf16[256,3200]{1,0:T(8,128)(2,1)S(1)} custom-call(bf16[40,80,1024]{2,1,0:T(8,128)(2,1)} %t_hbm.3, bf16[1024,192]{1,0:T(8,128)(2,1)S(1)} %copy-done.1), custom_call_target="tpu_custom_call" | custom-call | tf_op jit(solution)/shard_map/pallas_call | solution.py:180
  5.4 1.5 %reshape.12 = bf16[128,2,3200]{2,1,0:T(2,128)(2,1)} reshape(bf16[256,3200]{1,0:T(8,128)(2,1)S(1)} %shard_map.55) | data formatting | bytes 3276800 | tf_op jit(solution)/shard_map/reshape | solution.py:254
  7.0 11.5 %all-to-all-start = ((bf16[128,2,3200]{2,1,0:T(2,128)(2,1)}), bf16[128,2,3200]{2,1,0:T(2,128)(2,1)S(1)}, u32[]{:S(2)}, u32[]{:S(2)}) async-start(bf16[128,2,3200]{2,1,0:T(2,128)(2,1)} %reshape.12), calls=%async_computation | async-start | bytes 3276800 | tf_op jit(solution)/shard_map/all_to_all | solution.py:255
  18.4 0.0 copy-done
  18.5 1.1 %convolution_bitcast_fusion = f32[2,7,16]{2,0,1:T(2,128)S(1)} fusion(f32[16,7,64]{2,0,1:T(8,128)S(1)} %copy-done, f32[128,2,64]{2,1,0:T(2,128)} %constant.24.clone, s32[]{:T(128)S(6)} %select_n.4), kind=kOutput, calls=%fused_computation | convolution fusion | flops 172032 | bytes 30596 | tf_op jit(solution)/shard_map/ck,wjk->cjw/dot_general | solution.py:258
  19.6 0.1 broadcast_in_dim.3
  19.7 0.1 reshape_reshape.3.w_ref
  19.8 23.9 %all-to-all-done = bf16[128,2,3200]{2,1,0:T(2,128)(2,1)S(1)} async-done(((bf16[128,2,3200]{2,1,0:T(2,128)(2,1)}), bf16[128,2,3200]{2,1,0:T(2,128)(2,1)S(1)}, u32[]{:S(2)}, u32[]{:S(2)}) %all-to-all-start) | async-done | bytes 1638432 | tf_op jit(solution)/shard_map/all_to_all | solution.py:255
  43.7 0.6 reshape.13.x_ref
  44.4 12.0 %shard_map.56 = bf16[256,3200]{1,0:T(8,128)(2,1)S(1)} custom-call(bf16[256,3200]{1,0:T(8,128)(2,1)S(1)} %reshape.13.x_ref, f32[14,640]{1,0:T(8,128)S(1)} %reshape_reshape.3.w_ref), custom_call_target="tpu_custom_call" | custom-call | tf_op jit(solution)/shard_map/pallas_call | solution.py:137
  56.3 0.7 reshape.14
  57.0 30.1 %all_to_all.10 = bf16[128,2,3200]{2,1,0:T(2,128)(2,1)} all-to-all(bf16[128,2,3200]{2,1,0:T(2,128)(2,1)S(1)} %reshape.14), channel_id=1, replica_groups=mesh['freq'=8,'panel'=16] {'freq','panel'}, dimensions={0} | all-to-all | bytes 3276800 | tf_op jit(solution)/shard_map/all_to_all | solution.py:263
  87.1 0.0 copy-start.2
  87.2 3.8 %reshape.15.m_ref = bf16[256,3200]{1,0:T(8,128)(2,1)S(1)} reshape(bf16[128,2,3200]{2,1,0:T(2,128)(2,1)} %all_to_all.10) | data formatting | bytes 3276800 | tf_op jit(solution)/shard_map/reshape | solution.py:264
  90.9 0.0 copy-done.2
  90.9 5.1 %shard_map.57 = bf16[40,80,1024]{2,1,0:T(8,128)(2,1)} custom-call(bf16[256,3200]{1,0:T(8,128)(2,1)S(1)} %reshape.15.m_ref, bf16[40,80,1024]{2,1,0:T(8,128)(2,1)} %t_hbm.3, bf16[192,1024]{1,0:T(8,128)(2,1)S(1)} %copy-done.2), custom_call_target="tpu_custom_call" | custom-call | tf_op jit(solution)/shard_map/pallas_call | solution.py:221
  (1 shorter events, 0.0 us)
Async XLA Ops:
  0.0 18.4 %copy-start = (f32[16,7,64]{2,0,1:T(8,128)S(1)}, f32[16,7,64]{2,0,1:T(8,128)}, u32[]{:S(2)}) copy-start(f32[16,7,64]{2,0,1:T(8,128)} %param.6) | copy-start | bytes 86020
  0.0 1.0 %copy-start.1 = (bf16[1024,192]{1,0:T(8,128)(2,1)S(1)}, bf16[1024,192]{1,0:T(8,128)(2,1)}, u32[]{:S(2)}) copy-start(bf16[1024,192]{1,0:T(8,128)(2,1)} %constant.23.clone.f_ref) | copy-start | bytes 1179652
  7.0 36.8 %all-to-all-start = ((bf16[128,2,3200]{2,1,0:T(2,128)(2,1)}), bf16[128,2,3200]{2,1,0:T(2,128)(2,1)S(1)}, u32[]{:S(2)}, u32[]{:S(2)}) async-start(bf16[128,2,3200]{2,1,0:T(2,128)(2,1)} %reshape.12), calls=%async_computation | async-start | bytes 3276800 | tf_op jit(solution)/shard_map/all_to_all | solution.py:255
  87.1 3.8 %copy-start.2 = (bf16[192,1024]{1,0:T(8,128)(2,1)S(1)}, bf16[192,1024]{1,0:T(8,128)(2,1)}, u32[]{:S(2)}) copy-start(bf16[192,1024]{1,0:T(8,128)(2,1)} %constant.25.clone.i_ref) | copy-start | bytes 1179652

commit v4 on v3

--- a/solution.py
+++ b/solution.py
@@ -58,7 +58,8 @@
         base = pl.multiple_of(g * width, 128)
         for s in range(group):
             def read(q, tile):
-                return x_ref[q * pair:(q + 1) * pair, pl.ds(pl.multiple_of(base + tile * 128, 128), 128)].astype(f32)
+                lanes = pl.ds(pl.multiple_of(base + tile * 128, 128), 128)
+                return x_ref[q * n_panel:(q + 1) * n_panel, :, lanes].reshape(pair, 128).astype(f32)
             for t in range(tiles):
                 z_ref[t, pl.ds(g * group + s, pair, stride=rows), :] = gather(read, s, t)
         return 0
@@ -94,7 +95,7 @@
             else:
                 o_ref[NS:, (t - tiles) * 128:(t - tiles) * 128 + 128] = (-ob).astype(bf16)
     zero = jnp.zeros((8, 128), f32)
-    for t in range(2 * tiles):
+    for t in range(3 * tiles):
         f_ref[t, 0:8, :] = zero
         f_ref[t, 8 + NS:16 + NS, :] = zero
     for n in range(2 * width // step):
@@ -102,22 +103,26 @@
         o = jnp.dot(l_ref[...], o_ref[:, c], preferred_element_type=f32) * root
         pred = (o_ref[:NS, c].astype(f32) - o).astype(bf16).astype(f32)
         for h in range(step // 128):
-            f_ref[n * (step // 128) + h, 8:8 + NS, :] = pred[:, h * 128:h * 128 + 128]
+            t = n * (step // 128) + h
+            f_ref[t, 8:8 + NS, :] = pred[:, h * 128:h * 128 + 128]
+            if t >= tiles:
+                f_ref[t + tiles, 8:8 + NS, :] = f_ref[t - tiles, 8:8 + NS, :] + pred[:, h * 128:h * 128 + 128]
 
     rim = SPAN // 2
     for t in range(tiles):
-        weights = [jnp.broadcast_to(w_ref[i:i + 1, t * 128:t * 128 + 128], (rows, 128)) for i in range(2 * SPAN)]
+        weights = [jnp.broadcast_to(w_ref[i:i + 1, t * 128:t * 128 + 128], (rows, 128)) for i in range(3 * SPAN)]
+
         def match(p, _):
-            real = imag = None
+            sums = [None] * 3
             for j in range(SPAN):
                 at = pl.ds(p * rows + 8 - rim + j, rows)
-                a, b = f_ref[t, at, :], f_ref[tiles + t, at, :]
-                wr, wi = weights[j], weights[SPAN + j]
-                re, im = wr * a - wi * b, wr * b + wi * a
-                real, imag = (re, im) if real is None else (real + re, imag + im)
-            z_ref[t, pl.ds(pl.multiple_of(p * 2 * rows, 8), rows), :] = real
-            z_ref[t, pl.ds(pl.multiple_of(p * 2 * rows + rows, 8), rows), :] = imag
+                for i, plane in enumerate((2 * tiles + t, tiles + t, t)):
+                    term = weights[i * SPAN + j] * f_ref[plane, at, :]
+                    sums[i] = term if sums[i] is None else sums[i] + term
+            z_ref[t, pl.ds(pl.multiple_of(p * 2 * rows, 8), rows), :] = sums[0] - sums[1]
+            z_ref[t, pl.ds(pl.multiple_of(p * 2 * rows + rows, 8), rows), :] = sums[0] + sums[2]
             return 0
+
         lax.fori_loop(0, n_panel, match, 0)
 
     def join(g, _):
@@ -126,7 +131,8 @@
             return z_ref[tile, pl.ds(g * group + s, pair, stride=rows), :]
         for q in range(n_freq):
             for t in range(tiles):
-                y_ref[q * pair:(q + 1) * pair, pl.ds(pl.multiple_of(base + t * 128, 128), 128)] = gather(read, q, t).astype(bf16)
+                lanes = pl.ds(pl.multiple_of(base + t * 128, 128), 128)
+                y_ref[q * n_panel:(q + 1) * n_panel, :, lanes] = gather(read, q, t).astype(bf16).reshape(n_panel, 2, 128)
         return 0
     lax.fori_loop(0, groups, join, 0)
 
@@ -144,26 +150,53 @@
             pltpu.VMEM((NS, 2 * width), bf16),
             pltpu.VMEM((2 * NS, 2 * width), bf16),
             pltpu.VMEM((2 * NS, 2 * width), bf16),
-            pltpu.VMEM((2 * width // 128, NS + 16, 128), f32),
+            pltpu.VMEM((3 * width // 128, NS + 16, 128), f32),
         ],
         compiler_params=pltpu.CompilerParams(vmem_limit_bytes=22 << 20),
-    )(x, w)
-
-
-def first_kernel(t_hbm, f_ref, s_ref, t_ref, sem, *, group):
+    )(
+        pltpu.with_memory_space_constraint(x, pltpu.VMEM),
+        pltpu.with_memory_space_constraint(w, pltpu.VMEM),
+    )
+
+
+def first_kernel(t_hbm, f_hbm, tap_hbm, filt_hbm, s_ref, t_ref, w_ref, f_ref, tap_ref, filt_ref, sem, *, group):
     rows, cols, _ = t_ref.shape
     width, half = group * cols, group * cols // 2
-    used = f_ref.shape[1]
-
-    def copy(g):
+    used = f_ref.shape[1] // 2
+
+    def fetch(g):
         at = pl.ds(g * group, group)
         return pltpu.make_async_copy(t_hbm.at[at], t_ref.at[at], sem.at[g])
 
+    table = pltpu.make_async_copy(f_hbm, f_ref, sem.at[rows // group])
+    tap = pltpu.make_async_copy(tap_hbm.at[lax.axis_index(BOTH)], tap_ref, sem.at[rows // group + 1])
+    filt = pltpu.make_async_copy(filt_hbm, filt_ref, sem.at[rows // group + 2])
+    tap.start()
+    filt.start()
+    table.start()
     for g in range(rows // group):
-        copy(g).start()
-    s_ref[used:, :] = jnp.zeros((s_ref.shape[0] - used, s_ref.shape[1]), s_ref.dtype)
+        fetch(g).start()
+    s_ref[used:] = jnp.zeros((s_ref.shape[0] - used,) + s_ref.shape[1:], s_ref.dtype)
+    tap.wait()
+    filt.wait()
+    window = lax.broadcasted_iota(jnp.int32, (NWIN, w_ref.shape[1]), 0) * RWIN
+    place = lax.broadcasted_iota(jnp.int32, (NWIN, w_ref.shape[1]), 1) - window
+    inside = (place >= 0) & (place < RWIN)
+    for j in range(SPAN):
+        real, imag = (
+            jnp.sum(
+                jnp.where(inside, jnp.sum(filt_ref[j] * tap_ref[c : c + 1, :], 1, keepdims=True), 0.0),
+                0,
+                keepdims=True,
+            )
+            for c in range(2)
+        )
+        w_ref[j : j + 1, :] = real
+        w_ref[SPAN + j : SPAN + j + 1, :] = real + imag
+        w_ref[2 * SPAN + j : 2 * SPAN + j + 1, :] = imag - real
+    table.wait()
     for g in range(rows // group):
-        copy(g).wait()
+        fetch(g).wait()
         block = t_ref[g * group : (g + 1) * group].reshape(width, NT)
         out = jnp.concatenate(
             [
@@ -172,69 +205,75 @@
             ],
             0,
         )
-        s_ref[:used, g * width : (g + 1) * width] = out.astype(s_ref.dtype).T
-
-
-def first(traces, forward, n_all, group=8):
+        s_ref[:used, :, g * width : (g + 1) * width] = out.astype(s_ref.dtype).T.reshape(used, 2, width)
+
+
+def first(traces, forward, taps, filters, n_all, receivers, group=8):
     rows, cols, _ = traces.shape
+    hbm, vmem = pl.BlockSpec(memory_space=pltpu.HBM), pl.BlockSpec(memory_space=pltpu.VMEM)
     return pl.pallas_call(
         functools.partial(first_kernel, group=group),
-        out_shape=pltpu.VMEM((2 * n_all, rows * cols), jnp.bfloat16),
-        in_specs=[
-            pl.BlockSpec(memory_space=pltpu.HBM),
-            pl.BlockSpec(memory_space=pltpu.VMEM),
+        out_shape=(
+            pltpu.VMEM((n_all, 2, rows * cols), jnp.bfloat16),
+            pltpu.VMEM(traces.shape, jnp.bfloat16),
+            pltpu.VMEM((3 * SPAN, receivers), jnp.float32),
+        ),
+        in_specs=[hbm] * 4,
+        out_specs=(vmem, vmem, vmem),
+        scratch_shapes=[
+            pltpu.VMEM(forward.shape, jnp.bfloat16),
+            pltpu.VMEM(taps.shape[1:], jnp.float32),
+            pltpu.VMEM(filters.shape, jnp.float32),
+            pltpu.SemaphoreType.DMA((rows // group + 3,)),
         ],
-        out_specs=pl.BlockSpec(memory_space=pltpu.VMEM),
-        scratch_shapes=[pltpu.VMEM(traces.shape, jnp.bfloat16), pltpu.SemaphoreType.DMA((rows // group,))],
-        compiler_params=pltpu.CompilerParams(vmem_limit_bytes=20 << 20),
-    )(pltpu.with_memory_space_constraint(traces, pltpu.HBM), forward)
-
-
-def last_kernel(m_ref, t_hbm, i_ref, o_hbm, t_ref, o_ref, t_sem, sem, *, group, part):
+        compiler_params=pltpu.CompilerParams(vmem_limit_bytes=12 << 20),
+    )(
+        pltpu.with_memory_space_constraint(traces, pltpu.HBM),
+        pltpu.with_memory_space_constraint(forward, pltpu.HBM),
+        pltpu.with_memory_space_constraint(taps, pltpu.HBM),
+        pltpu.with_memory_space_constraint(filters, pltpu.HBM),
+    )
+
+
+def last_kernel(m_ref, t_ref, i_ref, o_hbm, o_ref, sem, *, group, part):
     rows, cols, _ = t_ref.shape
     width = group * cols
     used = i_ref.shape[0]
     scale = 1.0 / math.sqrt(NF)
-    steps = group // part
-    def copy(g, h):
-        at = pl.ds(g * group + h * part, part)
+
+    def send(at):
         return pltpu.make_async_copy(o_ref.at[at], o_hbm.at[at], sem)
-    def fetch(g):
-        at = pl.ds(g * group, group)
-        return pltpu.make_async_copy(t_hbm.at[at], t_ref.at[at], t_sem.at[g])
 
     for g in range(rows // group):
-        fetch(g).start()
-    for g in range(rows // group):
-        fetch(g).wait()
-        mt = m_ref[:used, g * width:(g + 1) * width].T
-        for h in range(steps):
-            acc = jnp.dot(mt[h * part * cols:(h + 1) * part * cols], i_ref[...], preferred_element_type=jnp.float32)
-            at = slice(g * group + h * part, g * group + (h + 1) * part)
+        m = m_ref[: used // 2, :, g * width : (g + 1) * width].reshape(used, width).T
+        for h in range(group // part):
+            acc = jnp.dot(
+                m[h * part * cols : (h + 1) * part * cols], i_ref[...], preferred_element_type=jnp.float32
+            )
+            at = pl.ds(g * group + h * part, part)
             t = t_ref[at].astype(jnp.float32)
             o_ref[at] = (t - (acc * scale).reshape(t.shape)).astype(o_ref.dtype)
-            copy(g, h).start()
+            send(at).start()
     pltpu.make_async_copy(o_ref, o_hbm, sem).wait()
 
 
 def last(m, traces, inverse, group=8, part=2):
+    vmem = pl.BlockSpec(memory_space=pltpu.VMEM)
     return pl.pallas_call(
         functools.partial(last_kernel, group=group, part=part),
         out_shape=jax.ShapeDtypeStruct(traces.shape, jnp.bfloat16),
-        in_specs=[
-            pl.BlockSpec(memory_space=pltpu.VMEM),
-            pl.BlockSpec(memory_space=pltpu.HBM),
-            pl.BlockSpec(memory_space=pltpu.VMEM),
-        ],
+        in_specs=[vmem, vmem, vmem],
         out_specs=pl.BlockSpec(memory_space=pltpu.HBM),
         scratch_shapes=[
             pltpu.VMEM(traces.shape, jnp.bfloat16),
-            pltpu.VMEM(traces.shape, jnp.bfloat16),
-            pltpu.SemaphoreType.DMA((traces.shape[0] // group,)),
             pltpu.SemaphoreType.DMA(()),
         ],
-        compiler_params=pltpu.CompilerParams(vmem_limit_bytes=24 << 20),
-    )(m, pltpu.with_memory_space_constraint(traces, pltpu.HBM), inverse)
+        compiler_params=pltpu.CompilerParams(vmem_limit_bytes=16 << 20),
+    )(
+        pltpu.with_memory_space_constraint(m, pltpu.VMEM),
+        pltpu.with_memory_space_constraint(traces, pltpu.VMEM),
+        inverse,
+    )
 
 
 def solution(mesh):
@@ -250,19 +289,18 @@
 
     def per_device(traces, filters):
         rows, cols, _ = traces.shape
-        spectra = first(traces, jnp.asarray(forward, jnp.bfloat16), n_all)
-        spectra = spectra.reshape(n_all, 2, rows * cols)
+        spectra, kept, reply = first(
+            traces,
+            jnp.asarray(forward, jnp.bfloat16),
+            jnp.asarray(taps),
+            filters.transpose(1, 0, 2),
+            n_all,
+            n_freq * cols,
+        )
         slices = lax.all_to_all(spectra, BOTH, split_axis=0, concat_axis=0, tiled=True)
-        me = lax.axis_index(BOTH)
-        wave = lax.dynamic_index_in_dim(jnp.asarray(taps), me, 0, keepdims=False)
-        reply = jnp.einsum("ck,wjk->cjw", wave, filters, precision=lax.Precision.HIGHEST)
-        reply = jnp.repeat(reply, RWIN, axis=2).reshape(2 * SPAN, n_freq * cols)
-        matched = middle(
-            slices.reshape(2 * n_all, rows * cols), reply, n_freq, n_panel, rows, cols
-        ).reshape(n_all, 2, rows * cols)
+        matched = middle(slices, reply, n_freq, n_panel, rows, cols)
         back = lax.all_to_all(matched, BOTH, split_axis=0, concat_axis=0, tiled=True)
-        back = back.reshape(2 * n_all, rows * cols)
-        return last(back, traces, jnp.asarray(inverse, jnp.bfloat16))
+        return last(back, kept, jnp.asarray(inverse, jnp.bfloat16))
 
     placed = (P("panel", "freq", None), P())
     return jax.shard_map(

time: 96.5 us -> 87.3 us (0.905)
  blocking collectives: 30.1 us -> 66.3 us
  waiting for transfers between devices: 23.9 us -> 0 us
  starting transfers between devices: 11.5 us -> 0 us
  local copies, waits for them, and re-layouts: 7.89 us -> 0.01 us
  matrix products: 1.12 us -> 0 us
    all_to_all x0 -> x1, blocking collectives: none -> 36.6 us  [per_device(): lax.all_to_all(spectra, BOTH, split_axis=0, concat_axis=0, tiled=True)]
    all_to_all x1 -> x0, waiting for transfers between devices: 23.9 us -> none  [per_device(): lax.all_to_all(spectra, BOTH, split_axis=0, concat_axis=0, tiled=True)]
    all_to_all x1 -> x0, starting transfers between devices: 11.5 us -> none  [per_device(): lax.all_to_all(spectra, BOTH, split_axis=0, concat_axis=0, tiled=True)]
    reshape x4 -> x0, local copies, waits for them, and re-layouts: 6.61 us -> none  [the longest x1 3.77 us: per_device(): back = back.reshape(2 * n_all, rows * cols)]
    pallas_call x1, Pallas kernels: 5.07 us -> 3.2 us  [last(): pl.pallas_call(functools.partial(last_kernel, group=group, part=part), ou...]
    dot_general x1 -> x0, matrix products: 1.12 us -> none  [per_device(): jnp.einsum('ck,wjk->cjw', wave, filters, precision=lax.Precision.HIGHEST)]
    pallas_call x1, Pallas kernels: 12 us -> 13 us  [middle(): pl.pallas_call(functools.partial(mid_kernel, n_freq=n_freq, n_panel=n_pan...]
    unnamed x6 -> x2, local copies, waits for them, and re-layouts: 1.06 us -> 0.01 us
  transfers between devices with their start and end apart: 1 -> 0, of which waited for: 1 -> 0; matrix products, arithmetic and copies ran while one was open for 1% -> 0% of each run, Pallas kernels for 0% -> 0%
where the time goes in v4:
time: 87.3 us; the launch traced here: 87.2 us
  blocking collectives  66.3 us (76%)
  Pallas kernels  20.9 us (24%)
    all_to_all x1, blocking collectives, per_device(): lax.all_to_all(spectra, BOTH, split_axis=0, concat_axis=0, tiled=True)  36.6 us
    all_to_all x1, blocking collectives, per_device(): lax.all_to_all(matched, BOTH, split_axis=0, concat_axis=0, tiled=True)  29.7 us
    pallas_call x1, Pallas kernels, middle(): pl.pallas_call(functools.partial(mid_kernel, n_freq=n_freq, n_panel=n_pan...  13 us
    pallas_call x1, Pallas kernels, first(): pl.pallas_call(functools.partial(first_kernel, group=group), out_shape=(p...  4.64 us
    pallas_call x1, Pallas kernels, last(): pl.pallas_call(functools.partial(last_kernel, group=group, part=part), ou...  3.2 us

profile of v4, /device:TPU:1, one launch (start us, length us, event | category | flops | bytes accessed | tf_op | source)
XLA Modules:
  0.0 87.2 jit_solution(7432145110490058494)
XLA Ops:
  0.0 4.6 %shard_map.55 = (bf16[128,2,3200]{2,1,0:T(2,128)(2,1)S(1)}, bf16[40,80,1024]{2,1,0:T(8,128)(2,1)S(1)}, f32[21,640]{1,0:T(8,128)S(1)}) custom-call(bf16[40,80,1024]{2,1,0:T(8,128)(2,1)} %t_hbm.1, bf16[1024,192]{1,0:T(8,128)(2,1)} %constant.6.clone.f_hbm, f32[128,2,64]{2,1,0:T(2,128)} %constant.7.clone.tap_hbm, f32[7,16,64]{2,1,0:T(8,128)} %bitcast.1), custom_call_target="tpu_custom_call" | custom-call | tf_op jit(solution)/shard_map/pallas_call | solution.py:214
  4.7 36.6 %all_to_all.10.x_ref = bf16[128,2,3200]{2,1,0:T(2,128)(2,1)S(1)} all-to-all(bf16[128,2,3200]{2,1,0:T(2,128)(2,1)S(1)} %get-tuple-element.8), channel_id=1, replica_groups=mesh['freq'=8,'panel'=16] {'freq','panel'}, dimensions={0} | all-to-all | bytes 3276800 | tf_op jit(solution)/shard_map/all_to_all | solution.py:300
  41.2 13.0 %shard_map.56 = bf16[128,2,3200]{2,1,0:T(2,128)(2,1)S(1)} custom-call(bf16[128,2,3200]{2,1,0:T(2,128)(2,1)S(1)} %all_to_all.10.x_ref, f32[21,640]{1,0:T(8,128)S(1)} %get-tuple-element.9.w_ref), custom_call_target="tpu_custom_call" | custom-call | tf_op jit(solution)/shard_map/pallas_call | solution.py:143
  54.3 0.0 copy-start
  54.3 29.7 %all_to_all.11.m_ref = bf16[128,2,3200]{2,1,0:T(2,128)(2,1)S(1)} all-to-all(bf16[128,2,3200]{2,1,0:T(2,128)(2,1)S(1)} %shard_map.56), channel_id=1, replica_groups=mesh['freq'=8,'panel'=16] {'freq','panel'}, dimensions={0} | all-to-all | bytes 3276800 | tf_op jit(solution)/shard_map/all_to_all | solution.py:302
  84.0 0.0 copy-done
  84.0 3.2 %shard_map.57 = bf16[40,80,1024]{2,1,0:T(8,128)(2,1)} custom-call(bf16[128,2,3200]{2,1,0:T(2,128)(2,1)S(1)} %all_to_all.11.m_ref, bf16[40,80,1024]{2,1,0:T(8,128)(2,1)S(1)} %get-tuple-element.10.t_ref, bf16[192,1024]{1,0:T(8,128)(2,1)S(1)} %copy-done), custom_call_target="tpu_custom_call" | custom-call | tf_op jit(solution)/shard_map/pallas_call | solution.py:262
Async XLA Ops:
  54.3 29.7 %copy-start = (bf16[192,1024]{1,0:T(8,128)(2,1)S(1)}, bf16[192,1024]{1,0:T(8,128)(2,1)}, u32[]{:S(2)}) copy-start(bf16[192,1024]{1,0:T(8,128)(2,1)} %constant.8.clone.i_ref) | copy-start | bytes 1179652

commit v5 on v4

--- a/solution.py
+++ b/solution.py
@@ -26,7 +26,7 @@
     return np.cos(angles), np.sin(angles)
 
 
-def mid_kernel(x_ref, w_ref, y_ref, z_ref, l_ref, r_ref, o_ref, f_ref, *, n_freq, n_panel, rows, cols):
+def mid_kernel(x_ref, w_ref, y_ref, z_ref, l_ref, r_ref, o_ref, f_ref, xs_ref, *, n_freq, n_panel, rows, cols):
     f32, bf16 = jnp.float32, jnp.bfloat16
     pair = 2 * n_panel
     width = n_freq * cols
@@ -54,14 +54,16 @@
                 value = v if value is None else jnp.where((lane >= d0) & (lane < d1), v, value)
         return value
 
+    for q in range(n_freq):
+        xs_ref[q * pair:(q + 1) * pair] = x_ref[q * n_panel:(q + 1) * n_panel].reshape(pair, rows * cols)
+
     def split(g, _):
         base = pl.multiple_of(g * width, 128)
         for s in range(group):
             def read(q, tile):
-                lanes = pl.ds(pl.multiple_of(base + tile * 128, 128), 128)
-                return x_ref[q * n_panel:(q + 1) * n_panel, :, lanes].reshape(pair, 128).astype(f32)
+                return xs_ref[q * pair:(q + 1) * pair, pl.ds(pl.multiple_of(base + tile * 128, 128), 128)]
             for t in range(tiles):
-                z_ref[t, pl.ds(g * group + s, pair, stride=rows), :] = gather(read, s, t)
+                z_ref[t, pl.ds(g * group + s, pair, stride=rows), :] = gather(read, s, t).astype(f32)
         return 0
     lax.fori_loop(0, groups, split, 0)
 
@@ -123,18 +125,19 @@
             z_ref[t, pl.ds(pl.multiple_of(p * 2 * rows + rows, 8), rows), :] = sums[0] + sums[2]
             return 0
 
-        lax.fori_loop(0, n_panel, match, 0)
+        lax.fori_loop(0, n_panel, match, 0, unroll=4)
 
     def join(g, _):
         base = pl.multiple_of(g * width, 128)
         def read(s, tile):
-            return z_ref[tile, pl.ds(g * group + s, pair, stride=rows), :]
+            return z_ref[tile, pl.ds(g * group + s, pair, stride=rows), :].astype(bf16)
         for q in range(n_freq):
             for t in range(tiles):
-                lanes = pl.ds(pl.multiple_of(base + t * 128, 128), 128)
-                y_ref[q * n_panel:(q + 1) * n_panel, :, lanes] = gather(read, q, t).astype(bf16).reshape(n_panel, 2, 128)
+                xs_ref[q * pair:(q + 1) * pair, pl.ds(pl.multiple_of(base + t * 128, 128), 128)] = gather(read, q, t)
         return 0
     lax.fori_loop(0, groups, join, 0)
+    for q in range(n_freq):
+        y_ref[q * n_panel:(q + 1) * n_panel] = xs_ref[q * pair:(q + 1) * pair].reshape(n_panel, 2, rows * cols)
 
 
 def middle(x, w, n_freq, n_panel, rows, cols):
@@ -151,8 +154,9 @@
             pltpu.VMEM((2 * NS, 2 * width), bf16),
             pltpu.VMEM((2 * NS, 2 * width), bf16),
             pltpu.VMEM((3 * width // 128, NS + 16, 128), f32),
+            pltpu.VMEM((2 * n_freq * n_panel, rows * cols), bf16),
         ],
-        compiler_params=pltpu.CompilerParams(vmem_limit_bytes=22 << 20),
+        compiler_params=pltpu.CompilerParams(vmem_limit_bytes=26 << 20),
     )(
         pltpu.with_memory_space_constraint(x, pltpu.VMEM),
         pltpu.with_memory_space_constraint(w, pltpu.VMEM),

time: 87.3 us -> 85.6 us (0.981)
  Pallas kernels: 20.9 us -> 19.1 us
    pallas_call x1, Pallas kernels: 13 us -> 11.2 us  [middle(): pl.pallas_call(functools.partial(mid_kernel, n_freq=n_freq, n_panel=n_pan...]
where the time goes in v5:
time: 85.6 us; the launch traced here: 85.4 us
  blocking collectives  66.3 us (77%)
  Pallas kernels  19.1 us (22%)
    all_to_all x1, blocking collectives, per_device(): lax.all_to_all(spectra, BOTH, split_axis=0, concat_axis=0, tiled=True)  36.6 us
    all_to_all x1, blocking collectives, per_device(): lax.all_to_all(matched, BOTH, split_axis=0, concat_axis=0, tiled=True)  29.7 us
    pallas_call x1, Pallas kernels, middle(): pl.pallas_call(functools.partial(mid_kernel, n_freq=n_freq, n_panel=n_pan...  11.2 us
    pallas_call x1, Pallas kernels, first(): pl.pallas_call(functools.partial(first_kernel, group=group), out_shape=(p...  4.64 us
    pallas_call x1, Pallas kernels, last(): pl.pallas_call(functools.partial(last_kernel, group=group, part=part), ou...  3.21 us

profile of v5, /device:TPU:1, one launch (start us, length us, event | category | flops | bytes accessed | tf_op | source)
XLA Modules:
  0.0 85.4 jit_solution(14447745619128250115)
XLA Ops:
  0.0 4.6 %shard_map.55 = (bf16[128,2,3200]{2,1,0:T(2,128)(2,1)S(1)}, bf16[40,80,1024]{2,1,0:T(8,128)(2,1)S(1)}, f32[21,640]{1,0:T(8,128)S(1)}) custom-call(bf16[40,80,1024]{2,1,0:T(8,128)(2,1)} %t_hbm.1, bf16[1024,192]{1,0:T(8,128)(2,1)} %constant.6.clone.f_hbm, f32[128,2,64]{2,1,0:T(2,128)} %constant.7.clone.tap_hbm, f32[7,16,64]{2,1,0:T(8,128)} %bitcast.1), custom_call_target="tpu_custom_call" | custom-call | tf_op jit(solution)/shard_map/pallas_call | solution.py:218
  4.7 36.6 %all_to_all.10.x_ref = bf16[128,2,3200]{2,1,0:T(2,128)(2,1)S(1)} all-to-all(bf16[128,2,3200]{2,1,0:T(2,128)(2,1)S(1)} %get-tuple-element.8), channel_id=1, replica_groups=mesh['freq'=8,'panel'=16] {'freq','panel'}, dimensions={0} | all-to-all | bytes 3276800 | tf_op jit(solution)/shard_map/all_to_all | solution.py:304
  41.2 11.2 %shard_map.56 = bf16[128,2,3200]{2,1,0:T(2,128)(2,1)S(1)} custom-call(bf16[128,2,3200]{2,1,0:T(2,128)(2,1)S(1)} %all_to_all.10.x_ref, f32[21,640]{1,0:T(8,128)S(1)} %get-tuple-element.9.w_ref), custom_call_target="tpu_custom_call" | custom-call | tf_op jit(solution)/shard_map/pallas_call | solution.py:146
  52.5 0.0 copy-start
  52.5 29.7 %all_to_all.11.m_ref = bf16[128,2,3200]{2,1,0:T(2,128)(2,1)S(1)} all-to-all(bf16[128,2,3200]{2,1,0:T(2,128)(2,1)S(1)} %shard_map.56), channel_id=1, replica_groups=mesh['freq'=8,'panel'=16] {'freq','panel'}, dimensions={0} | all-to-all | bytes 3276800 | tf_op jit(solution)/shard_map/all_to_all | solution.py:306
  82.2 0.0 copy-done
  82.2 3.2 %shard_map.57 = bf16[40,80,1024]{2,1,0:T(8,128)(2,1)} custom-call(bf16[128,2,3200]{2,1,0:T(2,128)(2,1)S(1)} %all_to_all.11.m_ref, bf16[40,80,1024]{2,1,0:T(8,128)(2,1)S(1)} %get-tuple-element.10.t_ref, bf16[192,1024]{1,0:T(8,128)(2,1)S(1)} %copy-done), custom_call_target="tpu_custom_call" | custom-call | tf_op jit(solution)/shard_map/pallas_call | solution.py:266
Async XLA Ops:
  52.5 29.7 %copy-start = (bf16[192,1024]{1,0:T(8,128)(2,1)S(1)}, bf16[192,1024]{1,0:T(8,128)(2,1)}, u32[]{:S(2)}) copy-start(bf16[192,1024]{1,0:T(8,128)(2,1)} %constant.8.clone.i_ref) | copy-start | bytes 1179652

commit v6 on v5

--- a/solution.py
+++ b/solution.py
@@ -26,93 +26,94 @@
     return np.cos(angles), np.sin(angles)
 
 
-def mid_kernel(x_ref, w_ref, y_ref, z_ref, l_ref, r_ref, o_ref, f_ref, xs_ref, *, n_freq, n_panel, rows, cols):
+def exchange(parts, lane, unit):
+    n, step = len(parts), 1
+    while step < n:
+        take = (lane // (unit * step)) % 2 == 1
+        parts = [jnp.where(take, parts[(j + step) % n], parts[j]) for j in range(n)]
+        step *= 2
+    return parts
+
+
+def mid_kernel(x_ref, w_ref, y_ref, z_ref, r_ref, o_ref, f_ref, xs_ref, *, n_freq, n_panel, rows, cols):
     f32, bf16 = jnp.float32, jnp.bfloat16
     pair = 2 * n_panel
     width = n_freq * cols
     tiles = width // 128
-    group = width // cols
-    groups = rows // group
+    unit = 128 // n_freq
     lane = lax.broadcasted_iota(jnp.int32, (pair, 128), 1)
     root = 1.0 / math.sqrt(NS)
 
-    def gather(read, outer, t):
-        value = None
-        for piece in range(group):
-            lo, hi = max(piece * cols, t * 128), min((piece + 1) * cols, t * 128 + 128)
-            if lo >= hi:
-                continue
-            src_lo = outer * cols + lo - piece * cols
-            src_hi = src_lo + hi - lo
-            for tile in range(src_lo // 128, (src_hi - 1) // 128 + 1):
-                a, b = max(src_lo, tile * 128), min(src_hi, tile * 128 + 128)
-                d0, d1 = a - src_lo + lo - t * 128, b - src_lo + lo - t * 128
-                shift = (d0 - (a - tile * 128)) % 128
-                v = read(piece, tile)
-                if shift:
-                    v = pltpu.roll(v, shift, 1)
-                value = v if value is None else jnp.where((lane >= d0) & (lane < d1), v, value)
-        return value
+    def words(q, g, u):
+        return slice(q * pair, (q + 1) * pair), pl.ds(pl.multiple_of(g * width + u * 128, 128), 128)
 
     for q in range(n_freq):
-        xs_ref[q * pair:(q + 1) * pair] = x_ref[q * n_panel:(q + 1) * n_panel].reshape(pair, rows * cols)
+        xs_ref[q * pair : (q + 1) * pair] = x_ref[q * n_panel : (q + 1) * n_panel].reshape(pair, rows * cols)
 
     def split(g, _):
-        base = pl.multiple_of(g * width, 128)
-        for s in range(group):
-            def read(q, tile):
-                return xs_ref[q * pair:(q + 1) * pair, pl.ds(pl.multiple_of(base + tile * 128, 128), 128)]
-            for t in range(tiles):
-                z_ref[t, pl.ds(g * group + s, pair, stride=rows), :] = gather(read, s, t).astype(f32)
+        for u in range(tiles):
+            sources = exchange([xs_ref[words(q, g, u)] for q in range(n_freq)], lane, unit)
+            for s in range(n_freq):
+                v = sources[-s % n_freq]
+                v = pltpu.roll(v, 128 - s * unit, 1) if s else v
+                z_ref[u, pl.ds(g * n_freq + s, pair, stride=rows), :] = v.astype(f32)
         return 0
-    lax.fori_loop(0, groups, split, 0)
-
-    def place(p, _):
-        row = pl.multiple_of(p * 2 * rows, 16)
+
+    lax.fori_loop(0, rows // n_freq, split, 0)
+
+    def place(q, _):
         for t in range(tiles):
-            z = z_ref[t, pl.ds(pl.multiple_of(p * 4 * rows, 8), 4 * rows), :]
-            re = jnp.concatenate([z[:rows], z[2 * rows:3 * rows]], 0)
-            im = jnp.concatenate([z[rows:2 * rows], z[3 * rows:]], 0)
-            c = slice(t * 128, t * 128 + 128); d = slice(width + t * 128, width + t * 128 + 128)
-            reb, imb = re.astype(bf16), im.astype(bf16)
-            l_ref[pl.ds(row, 2 * rows), c] = reb
-            l_ref[pl.ds(row, 2 * rows), d] = imb
-            r_ref[pl.ds(row, 2 * rows), c] = reb
-            r_ref[pl.ds(row, 2 * rows), d] = imb
-            r_ref[pl.ds(row + NS, 2 * rows), c] = (-im).astype(bf16)
-            r_ref[pl.ds(row + NS, 2 * rows), d] = reb
+            z = z_ref[t, pl.ds(pl.multiple_of(q * 4 * rows, 8), 4 * rows), :]
+            re = jnp.concatenate([z[:rows], z[2 * rows : 3 * rows]], 0)
+            im = jnp.concatenate([z[rows : 2 * rows], z[3 * rows :]], 0)
+            c, d = slice(t * 128, t * 128 + 128), slice(width + t * 128, width + t * 128 + 128)
+            for u in range(tiles):
+                part = slice(u * unit, (u + 1) * unit)
+                reb = re[part].astype(bf16)
+                row = pl.multiple_of(u * 128 + q * unit, unit)
+                r_ref[pl.ds(row, unit), c] = reb
+                r_ref[pl.ds(row, unit), d] = im[part].astype(bf16)
+                r_ref[pl.ds(row + NS, unit), c] = (-im[part]).astype(bf16)
+                r_ref[pl.ds(row + NS, unit), d] = reb
         return 0
-    lax.fori_loop(0, n_panel // 2, place, 0)
+
+    lax.fori_loop(0, n_freq, place, 0)
 
     step = 256
     for n in range(2 * width // step):
         c = slice(n * step, n * step + step)
-        o = jnp.dot(l_ref[...], r_ref[:, c], preferred_element_type=f32) * root
+        o = jnp.dot(r_ref[:NS, :], r_ref[:, c], preferred_element_type=f32) * root
         for h in range(step // 128):
             t = n * (step // 128) + h
-            ob = o[:, h * 128:h * 128 + 128]
-            o_ref[:NS, t * 128:t * 128 + 128] = ob.astype(bf16)
+            ob = o[:, h * 128 : h * 128 + 128]
+            o_ref[:NS, t * 128 : t * 128 + 128] = ob.astype(bf16)
             if t < tiles:
-                o_ref[NS:, width + t * 128:width + t * 128 + 128] = ob.astype(bf16)
+                o_ref[NS:, width + t * 128 : width + t * 128 + 128] = ob.astype(bf16)
             else:
-                o_ref[NS:, (t - tiles) * 128:(t - tiles) * 128 + 128] = (-ob).astype(bf16)
+                o_ref[NS:, (t - tiles) * 128 : (t - tiles) * 128 + 128] = (-ob).astype(bf16)
     zero = jnp.zeros((8, 128), f32)
     for t in range(3 * tiles):
         f_ref[t, 0:8, :] = zero
-        f_ref[t, 8 + NS:16 + NS, :] = zero
+        f_ref[t, 8 + NS : 16 + NS, :] = zero
     for n in range(2 * width // step):
         c = slice(n * step, n * step + step)
-        o = jnp.dot(l_ref[...], o_ref[:, c], preferred_element_type=f32) * root
+        o = jnp.dot(r_ref[:NS, :], o_ref[:, c], preferred_element_type=f32) * root
         pred = (o_ref[:NS, c].astype(f32) - o).astype(bf16).astype(f32)
         for h in range(step // 128):
             t = n * (step // 128) + h
-            f_ref[t, 8:8 + NS, :] = pred[:, h * 128:h * 128 + 128]
-            if t >= tiles:
-                f_ref[t + tiles, 8:8 + NS, :] = f_ref[t - tiles, 8:8 + NS, :] + pred[:, h * 128:h * 128 + 128]
+            for at in range(0, NS, unit):
+                u, q = at // 128, at % 128 // unit
+                dst = slice(8 + q * cols + u * unit, 8 + q * cols + (u + 1) * unit)
+                v = pred[at : at + unit, h * 128 : h * 128 + 128]
+                f_ref[t, dst, :] = v
+                if t >= tiles:
+                    f_ref[t + tiles, dst, :] = f_ref[t - tiles, dst, :] + v
 
     rim = SPAN // 2
     for t in range(tiles):
-        weights = [jnp.broadcast_to(w_ref[i:i + 1, t * 128:t * 128 + 128], (rows, 128)) for i in range(3 * SPAN)]
+        weights = [
+            jnp.broadcast_to(w_ref[i : i + 1, t * 128 : t * 128 + 128], (rows, 128)) for i in range(3 * SPAN)
+        ]
 
         def match(p, _):
             sums = [None] * 3
@@ -128,16 +129,21 @@
         lax.fori_loop(0, n_panel, match, 0, unroll=4)
 
     def join(g, _):
-        base = pl.multiple_of(g * width, 128)
-        def read(s, tile):
-            return z_ref[tile, pl.ds(g * group + s, pair, stride=rows), :].astype(bf16)
-        for q in range(n_freq):
-            for t in range(tiles):
-                xs_ref[q * pair:(q + 1) * pair, pl.ds(pl.multiple_of(base + t * 128, 128), 128)] = gather(read, q, t)
+        for u in range(tiles):
+            sources = []
+            for s in range(n_freq):
+                v = z_ref[u, pl.ds(g * n_freq + s, pair, stride=rows), :].astype(bf16)
+                sources.append(pltpu.roll(v, s * unit, 1) if s else v)
+            blocks = exchange(sources, lane, unit)
+            for q in range(n_freq):
+                xs_ref[words(q, g, u)] = blocks[-q % n_freq]
         return 0
-    lax.fori_loop(0, groups, join, 0)
+
+    lax.fori_loop(0, rows // n_freq, join, 0)
     for q in range(n_freq):
-        y_ref[q * n_panel:(q + 1) * n_panel] = xs_ref[q * pair:(q + 1) * pair].reshape(n_panel, 2, rows * cols)
+        y_ref[q * n_panel : (q + 1) * n_panel] = xs_ref[q * pair : (q + 1) * pair].reshape(
+            n_panel, 2, rows * cols
+        )
 
 
 def middle(x, w, n_freq, n_panel, rows, cols):
@@ -150,7 +156,6 @@
         out_specs=pl.BlockSpec(memory_space=pltpu.VMEM),
         scratch_shapes=[
             pltpu.VMEM((width // 128, 2 * NS, 128), f32),
-            pltpu.VMEM((NS, 2 * width), bf16),
             pltpu.VMEM((2 * NS, 2 * width), bf16),
             pltpu.VMEM((2 * NS, 2 * width), bf16),
             pltpu.VMEM((3 * width // 128, NS + 16, 128), f32),
@@ -165,8 +170,9 @@
 
 def first_kernel(t_hbm, f_hbm, tap_hbm, filt_hbm, s_ref, t_ref, w_ref, f_ref, tap_ref, filt_ref, sem, *, group):
     rows, cols, _ = t_ref.shape
-    width, half = group * cols, group * cols // 2
+    width, unit = group * cols, 128 // group
     used = f_ref.shape[1] // 2
+    block = lax.axis_index("freq")
 
     def fetch(g):
         at = pl.ds(g * group, group)
@@ -184,7 +190,8 @@
     tap.wait()
     filt.wait()
     window = lax.broadcasted_iota(jnp.int32, (NWIN, w_ref.shape[1]), 0) * RWIN
-    place = lax.broadcasted_iota(jnp.int32, (NWIN, w_ref.shape[1]), 1) - window
+    place = lax.broadcasted_iota(jnp.int32, (NWIN, w_ref.shape[1]), 1)
+    place = (place % 128) // unit * cols + place // 128 * unit + place % unit - window
     inside = (place >= 0) & (place < RWIN)
     for j in range(SPAN):
         real, imag = (
@@ -201,11 +208,16 @@
     table.wait()
     for g in range(rows // group):
         fetch(g).wait()
-        block = t_ref[g * group : (g + 1) * group].reshape(width, NT)
+        pieces = [
+            t_ref[g * group + (k + group - block) % group, u * unit : (u + 1) * unit]
+            for u in range(cols // unit)
+            for k in range(group)
+        ]
+        half = len(pieces) // 2
         out = jnp.concatenate(
             [
-                jnp.dot(part, f_ref[...], preferred_element_type=jnp.float32)
-                for part in (block[:half], block[half:])
+                jnp.dot(jnp.concatenate(part, 0), f_ref[...], preferred_element_type=jnp.float32)
+                for part in (pieces[:half], pieces[half:])
             ],
             0,
         )
@@ -241,8 +253,9 @@
 
 def last_kernel(m_ref, t_ref, i_ref, o_hbm, o_ref, sem, *, group, part):
     rows, cols, _ = t_ref.shape
-    width = group * cols
+    width, unit = group * cols, 128 // group
     used = i_ref.shape[0]
+    block = lax.axis_index("freq")
     scale = 1.0 / math.sqrt(NF)
 
     def send(at):
@@ -250,14 +263,18 @@
 
     for g in range(rows // group):
         m = m_ref[: used // 2, :, g * width : (g + 1) * width].reshape(used, width).T
-        for h in range(group // part):
-            acc = jnp.dot(
-                m[h * part * cols : (h + 1) * part * cols], i_ref[...], preferred_element_type=jnp.float32
-            )
-            at = pl.ds(g * group + h * part, part)
-            t = t_ref[at].astype(jnp.float32)
-            o_ref[at] = (t - (acc * scale).reshape(t.shape)).astype(o_ref.dtype)
-            send(at).start()
+        for h in range(0, group, part):
+            pieces = [
+                m[u * 128 + k * unit : u * 128 + (k + 1) * unit]
+                for k in range(h, h + part)
+                for u in range(cols // unit)
+            ]
+            acc = jnp.dot(jnp.concatenate(pieces, 0), i_ref[...], preferred_element_type=jnp.float32)
+            for k in range(part):
+                at = g * group + (h + k + group - block) % group
+                t = t_ref[at].astype(jnp.float32)
+                o_ref[at] = (t - acc[k * cols : (k + 1) * cols] * scale).astype(o_ref.dtype)
+                send(at).start()
     pltpu.make_async_copy(o_ref, o_hbm, sem).wait()
 
 

time: 85.6 us -> 83.9 us (0.980)
  Pallas kernels: 19.1 us -> 17.5 us
    pallas_call x1, Pallas kernels: 11.2 us -> 9.45 us  [middle(): pl.pallas_call(functools.partial(mid_kernel, n_freq=n_freq, n_panel=n_pan...]
where the time goes in v6:
time: 83.9 us; the launch traced here: 83.8 us
  blocking collectives  66.3 us (79%)
  Pallas kernels  17.5 us (21%)
    all_to_all x1, blocking collectives, per_device(): lax.all_to_all(spectra, BOTH, split_axis=0, concat_axis=0, tiled=True)  36.6 us
    all_to_all x1, blocking collectives, per_device(): lax.all_to_all(matched, BOTH, split_axis=0, concat_axis=0, tiled=True)  29.7 us
    pallas_call x1, Pallas kernels, middle(): pl.pallas_call(functools.partial(mid_kernel, n_freq=n_freq, n_panel=n_pan...  9.45 us
    pallas_call x1, Pallas kernels, first(): pl.pallas_call(functools.partial(first_kernel, group=group), out_shape=(p...  4.65 us
    pallas_call x1, Pallas kernels, last(): pl.pallas_call(functools.partial(last_kernel, group=group, part=part), ou...  3.37 us

profile of v6, /device:TPU:1, one launch (start us, length us, event | category | flops | bytes accessed | tf_op | source)
XLA Modules:
  0.0 83.8 jit_solution(6439750499863101593)
XLA Ops:
  0.0 4.6 %shard_map.55 = (bf16[128,2,3200]{2,1,0:T(2,128)(2,1)S(1)}, bf16[40,80,1024]{2,1,0:T(8,128)(2,1)S(1)}, f32[21,640]{1,0:T(8,128)S(1)}) custom-call(bf16[40,80,1024]{2,1,0:T(8,128)(2,1)} %t_hbm.1, bf16[1024,192]{1,0:T(8,128)(2,1)} %constant.6.clone.f_hbm, f32[128,2,64]{2,1,0:T(2,128)} %constant.7.clone.tap_hbm, f32[7,16,64]{2,1,0:T(8,128)} %bitcast.1), custom_call_target="tpu_custom_call" | custom-call | tf_op jit(solution)/shard_map/pallas_call | solution.py:230
  4.7 36.6 %all_to_all.10.x_ref = bf16[128,2,3200]{2,1,0:T(2,128)(2,1)S(1)} all-to-all(bf16[128,2,3200]{2,1,0:T(2,128)(2,1)S(1)} %get-tuple-element.8), channel_id=1, replica_groups=mesh['freq'=8,'panel'=16] {'freq','panel'}, dimensions={0} | all-to-all | bytes 3276800 | tf_op jit(solution)/shard_map/all_to_all | solution.py:321
  41.2 9.5 %shard_map.56 = bf16[128,2,3200]{2,1,0:T(2,128)(2,1)S(1)} custom-call(bf16[128,2,3200]{2,1,0:T(2,128)(2,1)S(1)} %all_to_all.10.x_ref, f32[21,640]{1,0:T(8,128)S(1)} %get-tuple-element.9.w_ref), custom_call_target="tpu_custom_call" | custom-call | tf_op jit(solution)/shard_map/pallas_call | solution.py:152
  50.7 0.0 copy-start
  50.7 29.7 %all_to_all.11.m_ref = bf16[128,2,3200]{2,1,0:T(2,128)(2,1)S(1)} all-to-all(bf16[128,2,3200]{2,1,0:T(2,128)(2,1)S(1)} %shard_map.56), channel_id=1, replica_groups=mesh['freq'=8,'panel'=16] {'freq','panel'}, dimensions={0} | all-to-all | bytes 3276800 | tf_op jit(solution)/shard_map/all_to_all | solution.py:323
  80.4 0.0 copy-done
  80.4 3.4 %shard_map.57 = bf16[40,80,1024]{2,1,0:T(8,128)(2,1)} custom-call(bf16[128,2,3200]{2,1,0:T(2,128)(2,1)S(1)} %all_to_all.11.m_ref, bf16[40,80,1024]{2,1,0:T(8,128)(2,1)S(1)} %get-tuple-element.10.t_ref, bf16[192,1024]{1,0:T(8,128)(2,1)S(1)} %copy-done), custom_call_target="tpu_custom_call" | custom-call | tf_op jit(solution)/shard_map/pallas_call | solution.py:283
Async XLA Ops:
  50.7 29.7 %copy-start = (bf16[192,1024]{1,0:T(8,128)(2,1)S(1)}, bf16[192,1024]{1,0:T(8,128)(2,1)}, u32[]{:S(2)}) copy-start(bf16[192,1024]{1,0:T(8,128)(2,1)} %constant.8.clone.i_ref) | copy-start | bytes 1179652

commit v7 on v6

--- a/solution.py
+++ b/solution.py
@@ -172,6 +172,7 @@
     rows, cols, _ = t_ref.shape
     width, unit = group * cols, 128 // group
     used = f_ref.shape[1] // 2
+    scale = 1.0 / math.sqrt(NF)
     block = lax.axis_index("freq")
 
     def fetch(g):
@@ -202,6 +203,7 @@
             )
             for c in range(2)
         )
+        real, imag = real * scale, imag * scale
         w_ref[j : j + 1, :] = real
         w_ref[SPAN + j : SPAN + j + 1, :] = real + imag
         w_ref[2 * SPAN + j : 2 * SPAN + j + 1, :] = imag - real
@@ -256,7 +258,6 @@
     width, unit = group * cols, 128 // group
     used = i_ref.shape[0]
     block = lax.axis_index("freq")
-    scale = 1.0 / math.sqrt(NF)
 
     def send(at):
         return pltpu.make_async_copy(o_ref.at[at], o_hbm.at[at], sem)
@@ -273,7 +274,7 @@
             for k in range(part):
                 at = g * group + (h + k + group - block) % group
                 t = t_ref[at].astype(jnp.float32)
-                o_ref[at] = (t - acc[k * cols : (k + 1) * cols] * scale).astype(o_ref.dtype)
+                o_ref[at] = (t - acc[k * cols : (k + 1) * cols]).astype(o_ref.dtype)
                 send(at).start()
     pltpu.make_async_copy(o_ref, o_hbm, sem).wait()
 

time: 83.9 us -> 83.9 us (level)
  no operation moved by 1% of the time
where the time goes in v7:
time: 83.9 us; the launch traced here: 83.8 us
  blocking collectives  66.3 us (79%)
  Pallas kernels  17.5 us (21%)
    all_to_all x1, blocking collectives, per_device(): lax.all_to_all(spectra, BOTH, split_axis=0, concat_axis=0, tiled=True)  36.6 us
    all_to_all x1, blocking collectives, per_device(): lax.all_to_all(matched, BOTH, split_axis=0, concat_axis=0, tiled=True)  29.7 us
    pallas_call x1, Pallas kernels, middle(): pl.pallas_call(functools.partial(mid_kernel, n_freq=n_freq, n_panel=n_pan...  9.45 us
    pallas_call x1, Pallas kernels, first(): pl.pallas_call(functools.partial(first_kernel, group=group), out_shape=(p...  4.65 us
    pallas_call x1, Pallas kernels, last(): pl.pallas_call(functools.partial(last_kernel, group=group, part=part), ou...  3.36 us

profile of v7, /device:TPU:1, one launch (start us, length us, event | category | flops | bytes accessed | tf_op | source)
XLA Modules:
  0.0 83.8 jit_solution(4799036176349341207)
XLA Ops:
  0.0 4.6 %shard_map.55 = (bf16[128,2,3200]{2,1,0:T(2,128)(2,1)S(1)}, bf16[40,80,1024]{2,1,0:T(8,128)(2,1)S(1)}, f32[21,640]{1,0:T(8,128)S(1)}) custom-call(bf16[40,80,1024]{2,1,0:T(8,128)(2,1)} %t_hbm.1, bf16[1024,192]{1,0:T(8,128)(2,1)} %constant.6.clone.f_hbm, f32[128,2,64]{2,1,0:T(2,128)} %constant.7.clone.tap_hbm, f32[7,16,64]{2,1,0:T(8,128)} %bitcast.1), custom_call_target="tpu_custom_call" | custom-call | tf_op jit(solution)/shard_map/pallas_call | solution.py:232
  4.7 36.6 %all_to_all.10.x_ref = bf16[128,2,3200]{2,1,0:T(2,128)(2,1)S(1)} all-to-all(bf16[128,2,3200]{2,1,0:T(2,128)(2,1)S(1)} %get-tuple-element.8), channel_id=1, replica_groups=mesh['freq'=8,'panel'=16] {'freq','panel'}, dimensions={0} | all-to-all | bytes 3276800 | tf_op jit(solution)/shard_map/all_to_all | solution.py:322
  41.2 9.5 %shard_map.56 = bf16[128,2,3200]{2,1,0:T(2,128)(2,1)S(1)} custom-call(bf16[128,2,3200]{2,1,0:T(2,128)(2,1)S(1)} %all_to_all.10.x_ref, f32[21,640]{1,0:T(8,128)S(1)} %get-tuple-element.9.w_ref), custom_call_target="tpu_custom_call" | custom-call | tf_op jit(solution)/shard_map/pallas_call | solution.py:152
  50.7 0.0 copy-start
  50.7 29.7 %all_to_all.11.m_ref = bf16[128,2,3200]{2,1,0:T(2,128)(2,1)S(1)} all-to-all(bf16[128,2,3200]{2,1,0:T(2,128)(2,1)S(1)} %shard_map.56), channel_id=1, replica_groups=mesh['freq'=8,'panel'=16] {'freq','panel'}, dimensions={0} | all-to-all | bytes 3276800 | tf_op jit(solution)/shard_map/all_to_all | solution.py:324
  80.4 0.0 copy-done
  80.4 3.4 %shard_map.57 = bf16[40,80,1024]{2,1,0:T(8,128)(2,1)} custom-call(bf16[128,2,3200]{2,1,0:T(2,128)(2,1)S(1)} %all_to_all.11.m_ref, bf16[40,80,1024]{2,1,0:T(8,128)(2,1)S(1)} %get-tuple-element.10.t_ref, bf16[192,1024]{1,0:T(8,128)(2,1)S(1)} %copy-done), custom_call_target="tpu_custom_call" | custom-call | tf_op jit(solution)/shard_map/pallas_call | solution.py:284
Async XLA Ops:
  50.7 29.7 %copy-start = (bf16[192,1024]{1,0:T(8,128)(2,1)S(1)}, bf16[192,1024]{1,0:T(8,128)(2,1)}, u32[]{:S(2)}) copy-start(bf16[192,1024]{1,0:T(8,128)(2,1)} %constant.8.clone.i_ref) | copy-start | bytes 1179652
